TPU v7x, 256 devices: a whole 4x4x8 slice. The times are simulated.
256 devices in a mesh: gx: 4 (over y), gy: 8 (over x, core), gz: 8 (over z).
Axes of the slice: x: 4, y: 4, z: 8, core: 2. Of those that a mesh axis runs over, the one named last changes fastest.
Arguments:
- old_pos: float32 [3, 4, 8, 8, 1536], P(None, 'gx', 'gy', 'gz'), may hold values from -6 to 6
- displacement: float32 [3, 4, 8, 8, 1536], P(None, 'gx', 'gy', 'gz'), may hold values from -0.3 to 0.3
- inv_mass: float32 [4, 8, 8, 1536], P('gx', 'gy', 'gz'), may hold values from 0.0625 to 1
- bond_head: int32 [4, 8, 8, 1024], P('gx', 'gy', 'gz'), may hold values from 0 to 1535, as said below
- bond_tail: int32 [4, 8, 8, 1024], P('gx', 'gy', 'gz'), may hold values from 0 to 1967, as said below
- send_list: int32 [4, 8, 8, 16], P('gx', 'gy', 'gz'), may hold values from 0 to 1535, as said below
Outputs:
- new_pos: float32 [3, 4, 8, 8, 1536], P(None, 'gx', 'gy', 'gz')
- multipliers: float32 [4, 8, 8, 1024], P('gx', 'gy', 'gz')
Inputs may be any that keep to these rules, and one draw needn't show every extreme that they name: `bond_head`: distinct atoms of the owning domain; no atom is the first atom of two constraints. `bond_tail`: below 1536: an atom of the owning domain other than the constraint's first atom, never in send_list; otherwise a slot 1536 + block * 16 + entry with block in 0..26 other than 13, distinct within a domain; 192 constraints of each domain use such slots. `send_list`: distinct atoms of the domain; a send atom is never a constraint's first atom and never a local second atom.
All inputs are finite; a program needn't handle non-finite values.
Results may differ from a plain program's by a relative error of at most 0.0011.
Values sent between devices are 32-bit elements; how exact they have to be, the bound alone decides.
A program may use at most 64 MiB of HBM per device.

v0:
```python
import jax
import jax.numpy as jnp
from jax import lax
from jax.sharding import PartitionSpec as P

ORDER = 4


def with_halo(value, sides, width):
    for axis, dim in sides:
        devices, length = (lax.axis_size(axis), value.shape[dim])
        up = [(i, (i + 1) % devices) for i in range(devices)]
        down = [(j, i) for i, j in up]
        last = lax.slice_in_dim(value, length - width, length, axis=dim)
        leading = lax.slice_in_dim(value, 0, width, axis=dim)
        before = lax.ppermute(last, axis, up)
        after = lax.ppermute(leading, axis, down)
        value = jnp.concatenate([before, value, after], axis=dim)
    return value


def gather_back(returned):
    widened = with_halo(returned, (("gx", 1), ("gy", 2), ("gz", 3)), 1)
    return jnp.sum(widened[:, ::2, ::2, ::2, :], axis=(1, 2, 3))


def per_device(old_pos, displacement, inv_mass, bond_head, bond_tail, send_list):
    atom_count = old_pos.shape[-1]
    bond_count = bond_head.shape[-1]
    send_count = send_list.shape[-1]
    old_local = old_pos.reshape(3, atom_count)
    move_local = displacement.reshape(3, atom_count)
    mass_local = inv_mass.reshape(1, atom_count)
    head_atom = bond_head.reshape(bond_count)
    tail_atom = bond_tail.reshape(bond_count)
    outbound = send_list.reshape(send_count)
    wide_count = 27 * send_count
    packed = jnp.concatenate(
        [old_local[:, outbound], move_local[:, outbound], mass_local[:, outbound]], axis=0
    )
    arrived = with_halo(
        packed.reshape(7, 1, 1, 1, send_count), (("gx", 1), ("gy", 2), ("gz", 3)), 1
    )
    arrived = arrived.reshape(7, wide_count)
    pos_local = old_local + move_local
    ext_old = jnp.concatenate([old_local, arrived[0:3]], axis=1)
    ext_new = jnp.concatenate([pos_local, arrived[0:3] + arrived[3:6]], axis=1)
    ext_mass = jnp.concatenate([mass_local, arrived[6:7]], axis=1)
    bond_old = ext_old[:, head_atom] - ext_old[:, tail_atom]
    length = jnp.maximum(jnp.sqrt(jnp.sum(bond_old * bond_old, axis=0)), 0.5)
    direction = bond_old / length
    bond_scale = 1.0 / jnp.sqrt(ext_mass[0, head_atom] + ext_mass[0, tail_atom])

    def spread(values):
        weighted = bond_scale * values * direction
        buffer = jnp.zeros((3, atom_count + wide_count), jnp.float32)
        buffer = buffer.at[:, head_atom].add(weighted).at[:, tail_atom].add(-weighted)
        incoming = gather_back(buffer[:, atom_count:].reshape(3, 3, 3, 3, send_count))
        local_sum = buffer[:, :atom_count].at[:, outbound].add(incoming)
        return mass_local * local_sum

    def couple(values):
        shift_vec = spread(values)
        remote = with_halo(
            shift_vec[:, outbound].reshape(3, 1, 1, 1, send_count),
            (("gx", 1), ("gy", 2), ("gz", 3)),
            1,
        )
        extended = jnp.concatenate([shift_vec, remote.reshape(3, wide_count)], axis=1)
        return values - bond_scale * jnp.sum(
            direction * (extended[:, head_atom] - extended[:, tail_atom]), axis=0
        )

    def expand(right_side):
        solution = right_side
        series = right_side
        for sweep in range(ORDER):
            series = couple(series)
            solution = solution + series
        return solution

    right_one = bond_scale * (
        jnp.sum(direction * (ext_new[:, head_atom] - ext_new[:, tail_atom]), axis=0) - length
    )
    sol_one = expand(right_one)
    pos_local = pos_local - spread(sol_one)
    moved = with_halo(
        pos_local[:, outbound].reshape(3, 1, 1, 1, send_count), (("gx", 1), ("gy", 2), ("gz", 3)), 1
    )
    ext_moved = jnp.concatenate([pos_local, moved.reshape(3, wide_count)], axis=1)
    stretch = ext_moved[:, head_atom] - ext_moved[:, tail_atom]
    current = jnp.sum(stretch * stretch, axis=0)
    target = jnp.sqrt(jnp.maximum(2.0 * length * length - current, 0.5 * length * length))
    sol_two = expand(bond_scale * (length - target))
    pos_local = pos_local - spread(sol_two)
    return (pos_local.reshape(old_pos.shape), (sol_one + sol_two).reshape(bond_head.shape))


def solution(mesh):
    return jax.shard_map(
        per_device,
        mesh=mesh,
        in_specs=(
            P(None, "gx", "gy", "gz", None),
            P(None, "gx", "gy", "gz", None),
            P("gx", "gy", "gz", None),
            P("gx", "gy", "gz", None),
            P("gx", "gy", "gz", None),
            P("gx", "gy", "gz", None),
        ),
        out_specs=(P(None, "gx", "gy", "gz", None), P("gx", "gy", "gz", None)),
        check_vma=False,
    )
```

profile of v0, /device:TPU:24, one launch (start us, length us, event | category | flops | bytes accessed | tf_op | source)
XLA Modules:
  0.0 593.3 jit_solution(12159181414125831405)
XLA Ops:
  15.6 4.0 collective-permute-start.5
  29.1 4.0 gather_fusion.8
  37.3 6.5 %gather_fusion.4 = f32[1024]{0:T(1024)S(1)} fusion(f32[1,1968]{1,0:T(1,128)S(1)} %pad_maximum_fusion.83, s32[1024]{0:T(1024)S(1)} %bitcast.84), kind=kCustom, calls=%fused_computation.4 | custom fusion | bytes 16384 | tf_op jit(solution)/shard_map/gather | solution.py:52
  43.8 6.5 %gather_fusion.3 = f32[1024]{0:T(1024)S(1)} fusion(f32[1,1968]{1,0:T(1,128)S(1)} %pad_maximum_fusion.83, s32[1024]{0:T(1024)S(1)} %bitcast.85), kind=kCustom, calls=%fused_computation.3 | custom fusion | bytes 16384 | tf_op jit(solution)/shard_map/gather | solution.py:52
  51.9 6.9 %scatter_custom_fusion = f32[3,1968]{0,1:T(8,128)S(1)} fusion(s32[1024]{0:T(1024)S(1)} %bitcast.184, f32[]{:T(128)} %constant.6.clone.1, f32[1024]{0:T(1024)S(1)} %get-tuple-element.18, f32[1024,3]{1,0:T(8,128)S(1)} %get-tuple-element.22, f32[1024]{0:T(1024)S(1)} %sqrt_maximum_fusion), kind=kCustom, calls=%fused_computation.128 | custom fusion | flops 9216 | bytes 556100 | tf_op jit(solution)/shard_map/scatter-add | solution.py:57
  58.8 7.1 %scatter_custom_fusion.1 = f32[3,1968]{0,1:T(8,128)S(1)} fusion(f32[3,1968]{0,1:T(8,128)S(1)} %scatter_custom_fusion, s32[1024]{0:T(1024)S(1)} %bitcast.173, f32[1024]{0:T(1024)S(1)} %get-tuple-element.18, f32[1024,3]{1,0:T(8,128)S(1)} %get-tuple-element.22, f32[1024]{0:T(1024)S(1)} %sqrt_maximum_fusion), kind=kCustom, calls=%fused_computation.97 | custom fusion | flops 12288 | bytes 556096 | tf_op jit(solution)/shard_map/scatter-add | solution.py:57
  101.5 4.0 gather_fusion.11
  105.6 4.0 gather_fusion.10
  110.0 6.9 %scatter_custom_fusion.3 = f32[3,1968]{0,1:T(8,128)S(1)} fusion(s32[1024]{0:T(1024)S(1)} %bitcast.185, f32[]{:T(128)} %constant.6.clone.1, f32[1024]{0:T(1024)S(1)} %fusion.89, f32[1024,3]{1,0:T(8,128)S(1)} %get-tuple-element.22, f32[1024]{0:T(1024)S(1)} %sqrt_maximum_fusion), kind=kCustom, calls=%fused_computation.126 | custom fusion | flops 9216 | bytes 556100 | tf_op jit(solution)/shard_map/scatter-add | solution.py:57
  117.0 7.1 %scatter_custom_fusion.4 = f32[3,1968]{0,1:T(8,128)S(1)} fusion(f32[3,1968]{0,1:T(8,128)S(1)} %scatter_custom_fusion.3, s32[1024]{0:T(1024)S(1)} %bitcast.174, f32[1024]{0:T(1024)S(1)} %fusion.89, f32[1024,3]{1,0:T(8,128)S(1)} %get-tuple-element.22, f32[1024]{0:T(1024)S(1)} %sqrt_maximum_fusion), kind=kCustom, calls=%fused_computation.95 | custom fusion | flops 12288 | bytes 556096 | tf_op jit(solution)/shard_map/scatter-add | solution.py:57
  158.3 4.0 gather_fusion.14
  162.3 4.0 gather_fusion.13
  166.8 6.9 %scatter_custom_fusion.6 = f32[3,1968]{0,1:T(8,128)S(1)} fusion(s32[1024]{0:T(1024)S(1)} %bitcast.186, f32[]{:T(128)} %constant.6.clone.1, f32[1024]{0:T(1024)S(1)} %fusion.92, f32[1024,3]{1,0:T(8,128)S(1)} %get-tuple-element.22, f32[1024]{0:T(1024)S(1)} %sqrt_maximum_fusion), kind=kCustom, calls=%fused_computation.124 | custom fusion | flops 9216 | bytes 556100 | tf_op jit(solution)/shard_map/scatter-add | solution.py:57
  173.7 7.1 %scatter_custom_fusion.7 = f32[3,1968]{0,1:T(8,128)S(1)} fusion(f32[3,1968]{0,1:T(8,128)S(1)} %scatter_custom_fusion.6, s32[1024]{0:T(1024)S(1)} %bitcast.175, f32[1024]{0:T(1024)S(1)} %fusion.92, f32[1024,3]{1,0:T(8,128)S(1)} %get-tuple-element.22, f32[1024]{0:T(1024)S(1)} %sqrt_maximum_fusion), kind=kCustom, calls=%fused_computation.93 | custom fusion | flops 12288 | bytes 556096 | tf_op jit(solution)/shard_map/scatter-add | solution.py:57
  215.0 4.0 gather_fusion.17
  219.0 4.0 gather_fusion.16
  223.5 6.9 %scatter_custom_fusion.9 = f32[3,1968]{0,1:T(8,128)S(1)} fusion(s32[1024]{0:T(1024)S(1)} %bitcast.187, f32[]{:T(128)} %constant.6.clone.1, f32[1024]{0:T(1024)S(1)} %fusion.87, f32[1024,3]{1,0:T(8,128)S(1)} %get-tuple-element.22, f32[1024]{0:T(1024)S(1)} %sqrt_maximum_fusion), kind=kCustom, calls=%fused_computation.122 | custom fusion | flops 9216 | bytes 556100 | tf_op jit(solution)/shard_map/scatter-add | solution.py:57
  230.4 7.1 %scatter_custom_fusion.10 = f32[3,1968]{0,1:T(8,128)S(1)} fusion(f32[3,1968]{0,1:T(8,128)S(1)} %scatter_custom_fusion.9, s32[1024]{0:T(1024)S(1)} %bitcast.176, f32[1024]{0:T(1024)S(1)} %fusion.87, f32[1024,3]{1,0:T(8,128)S(1)} %get-tuple-element.22, f32[1024]{0:T(1024)S(1)} %sqrt_maximum_fusion), kind=kCustom, calls=%fused_computation.91 | custom fusion | flops 12288 | bytes 556096 | tf_op jit(solution)/shard_map/scatter-add | solution.py:57
  271.0 4.0 gather_fusion.20
  275.0 4.0 gather_fusion.19
  279.5 6.9 %scatter_custom_fusion.12 = f32[3,1968]{0,1:T(8,128)S(1)} fusion(s32[1024]{0:T(1024)S(1)} %bitcast.188, f32[]{:T(128)} %constant.6.clone.1, f32[1024]{0:T(1024)S(1)} %add_multiply_fusion.1, f32[1024,3]{1,0:T(8,128)S(1)} %get-tuple-element.22, f32[1024]{0:T(1024)S(1)} %sqrt_maximum_fusion), kind=kCustom, calls=%fused_computation.120 | custom fusion | flops 9216 | bytes 556100 | tf_op jit(solution)/shard_map/scatter-add | solution.py:57
  286.5 7.1 %scatter_custom_fusion.13 = f32[3,1968]{0,1:T(8,128)S(1)} fusion(f32[3,1968]{0,1:T(8,128)S(1)} %scatter_custom_fusion.12, s32[1024]{0:T(1024)S(1)} %bitcast.177, f32[1024]{0:T(1024)S(1)} %add_multiply_fusion.1, f32[1024,3]{1,0:T(8,128)S(1)} %get-tuple-element.22, f32[1024]{0:T(1024)S(1)} %sqrt_maximum_fusion), kind=kCustom, calls=%fused_computation.89 | custom fusion | flops 12288 | bytes 556096 | tf_op jit(solution)/shard_map/scatter-add | solution.py:57
  338.3 6.9 %scatter_custom_fusion.15 = f32[3,1968]{0,1:T(8,128)S(1)} fusion(s32[1024]{0:T(1024)S(1)} %bitcast.189, f32[]{:T(128)} %constant.6.clone.1, f32[1024]{0:T(1024)S(1)} %get-tuple-element.16, f32[1024,3]{1,0:T(8,128)S(1)} %get-tuple-element.22, f32[1024]{0:T(1024)S(1)} %sqrt_maximum_fusion), kind=kCustom, calls=%fused_computation.118 | custom fusion | flops 9216 | bytes 556100 | tf_op jit(solution)/shard_map/scatter-add | solution.py:57
  345.2 7.1 %scatter_custom_fusion.16 = f32[3,1968]{0,1:T(8,128)S(1)} fusion(f32[3,1968]{0,1:T(8,128)S(1)} %scatter_custom_fusion.15, s32[1024]{0:T(1024)S(1)} %bitcast.178, f32[1024]{0:T(1024)S(1)} %get-tuple-element.16, f32[1024,3]{1,0:T(8,128)S(1)} %get-tuple-element.22, f32[1024]{0:T(1024)S(1)} %sqrt_maximum_fusion), kind=kCustom, calls=%fused_computation.87 | custom fusion | flops 12288 | bytes 556096 | tf_op jit(solution)/shard_map/scatter-add | solution.py:57
  393.8 6.9 %scatter_custom_fusion.18 = f32[3,1968]{0,1:T(8,128)S(1)} fusion(s32[1024]{0:T(1024)S(1)} %bitcast.190, f32[]{:T(128)} %constant.6.clone.1, f32[1024]{0:T(1024)S(1)} %fusion.90, f32[1024,3]{1,0:T(8,128)S(1)} %get-tuple-element.22, f32[1024]{0:T(1024)S(1)} %sqrt_maximum_fusion), kind=kCustom, calls=%fused_computation.116 | custom fusion | flops 9216 | bytes 556100 | tf_op jit(solution)/shard_map/scatter-add | solution.py:57
  400.8 7.1 %scatter_custom_fusion.19 = f32[3,1968]{0,1:T(8,128)S(1)} fusion(f32[3,1968]{0,1:T(8,128)S(1)} %scatter_custom_fusion.18, s32[1024]{0:T(1024)S(1)} %bitcast.179, f32[1024]{0:T(1024)S(1)} %fusion.90, f32[1024,3]{1,0:T(8,128)S(1)} %get-tuple-element.22, f32[1024]{0:T(1024)S(1)} %sqrt_maximum_fusion), kind=kCustom, calls=%fused_computation.85 | custom fusion | flops 12288 | bytes 556096 | tf_op jit(solution)/shard_map/scatter-add | solution.py:57
  449.3 6.9 %scatter_custom_fusion.21 = f32[3,1968]{0,1:T(8,128)S(1)} fusion(s32[1024]{0:T(1024)S(1)} %bitcast.191, f32[]{:T(128)} %constant.6.clone.1, f32[1024]{0:T(1024)S(1)} %fusion.93, f32[1024,3]{1,0:T(8,128)S(1)} %get-tuple-element.22, f32[1024]{0:T(1024)S(1)} %sqrt_maximum_fusion), kind=kCustom, calls=%fused_computation.114 | custom fusion | flops 9216 | bytes 556100 | tf_op jit(solution)/shard_map/scatter-add | solution.py:57
  456.3 7.1 %scatter_custom_fusion.22 = f32[3,1968]{0,1:T(8,128)S(1)} fusion(f32[3,1968]{0,1:T(8,128)S(1)} %scatter_custom_fusion.21, s32[1024]{0:T(1024)S(1)} %bitcast.180, f32[1024]{0:T(1024)S(1)} %fusion.93, f32[1024,3]{1,0:T(8,128)S(1)} %get-tuple-element.22, f32[1024]{0:T(1024)S(1)} %sqrt_maximum_fusion), kind=kCustom, calls=%fused_computation.83 | custom fusion | flops 12288 | bytes 556096 | tf_op jit(solution)/shard_map/scatter-add | solution.py:57
  504.1 6.9 %scatter_custom_fusion.24 = f32[3,1968]{0,1:T(8,128)S(1)} fusion(s32[1024]{0:T(1024)S(1)} %bitcast.192, f32[]{:T(128)} %constant.6.clone.1, f32[1024]{0:T(1024)S(1)} %fusion.88, f32[1024,3]{1,0:T(8,128)S(1)} %get-tuple-element.22, f32[1024]{0:T(1024)S(1)} %sqrt_maximum_fusion), kind=kCustom, calls=%fused_computation.112 | custom fusion | flops 9216 | bytes 556100 | tf_op jit(solution)/shard_map/scatter-add | solution.py:57
  511.1 7.1 %scatter_custom_fusion.25 = f32[3,1968]{0,1:T(8,128)S(1)} fusion(f32[3,1968]{0,1:T(8,128)S(1)} %scatter_custom_fusion.24, s32[1024]{0:T(1024)S(1)} %bitcast.181, f32[1024]{0:T(1024)S(1)} %fusion.88, f32[1024,3]{1,0:T(8,128)S(1)} %get-tuple-element.22, f32[1024]{0:T(1024)S(1)} %sqrt_maximum_fusion), kind=kCustom, calls=%fused_computation.81 | custom fusion | flops 12288 | bytes 556096 | tf_op jit(solution)/shard_map/scatter-add | solution.py:57
  560.0 6.9 %scatter_custom_fusion.27 = f32[3,1968]{0,1:T(8,128)S(1)} fusion(s32[1024]{0:T(1024)S(1)} %bitcast.193, f32[]{:T(128)} %constant.6.clone.1, f32[1024]{0:T(1024)S(1)} %add_multiply_fusion, f32[1024,3]{1,0:T(8,128)S(1)} %get-tuple-element.22, f32[1024]{0:T(1024)S(1)} %sqrt_maximum_fusion), kind=kCustom, calls=%fused_computation.110 | custom fusion | flops 9216 | bytes 556100 | tf_op jit(solution)/shard_map/scatter-add | solution.py:57
  567.0 7.1 %scatter_custom_fusion.28 = f32[3,1968]{0,1:T(8,128)S(1)} fusion(f32[3,1968]{0,1:T(8,128)S(1)} %scatter_custom_fusion.27, s32[1024]{0:T(1024)S(1)} %bitcast.182, f32[1024]{0:T(1024)S(1)} %add_multiply_fusion, f32[1024,3]{1,0:T(8,128)S(1)} %get-tuple-element.22, f32[1024]{0:T(1024)S(1)} %sqrt_maximum_fusion), kind=kCustom, calls=%fused_computation.79 | custom fusion | flops 12288 | bytes 556096 | tf_op jit(solution)/shard_map/scatter-add | solution.py:57
  (537 shorter events, 397.2 us)
Async XLA Ops:
  15.3 6.2 %collective-permute-start.4 = (f32[7,3,3,1,16]{4,0,3,2,1:T(8,128)S(1)}, f32[7,3,3,1,16]{4,0,3,2,1:T(8,128)S(1)}, u32[]{:S(2)}, u32[]{:S(2)}) collective-permute-start(f32[7,3,3,1,16]{4,0,3,2,1:T(8,128)S(1)} %pad_maximum_fusion.41), channel_id=1, source_target_pairs={{0,1},{1,2},{2,3},{3,4},{4,5},{5,6},{6,7},{7,0},{8,9},{9,10},{10,1... | collective-permute-start | bytes 12104 | tf_op jit(solution)/shard_map/ppermute | solution.py:16
  15.6 6.0 %collective-permute-start.5 = (f32[7,3,3,1,16]{4,0,3,2,1:T(8,128)S(1)}, f32[7,3,3,1,16]{4,0,3,2,1:T(8,128)S(1)}, u32[]{:S(2)}, u32[]{:S(2)}) collective-permute-start(f32[7,3,3,1,16]{4,0,3,2,1:T(8,128)S(1)} %pad_maximum_fusion.41), channel_id=1, source_target_pairs={{1,0},{2,1},{3,2},{4,3},{5,4},{6,5},{7,6},{0,7},{9,8},{10,9},{11,1... | collective-permute-start | bytes 12104 | tf_op jit(solution)/shard_map/ppermute | solution.py:17
  66.7 5.3 collective-permute-start.7
  76.7 5.3 collective-permute-start.10
  76.8 5.2 collective-permute-start.11
  93.6 5.1 collective-permute-start.16
  124.6 5.2 collective-permute-start.19
  134.4 5.3 collective-permute-start.22
  151.9 5.0 collective-permute-start.28
  181.6 5.4 collective-permute-start.31
  191.6 5.3 collective-permute-start.34
  208.6 5.0 collective-permute-start.40
  238.0 5.1 collective-permute-start.43
  247.9 5.3 collective-permute-start.46
  264.6 5.0 collective-permute-start.52
  294.3 5.4 collective-permute-start.55
  304.4 5.3 collective-permute-start.58
  324.1 5.0 collective-permute-start.64
  352.8 5.1 collective-permute-start.67
  362.7 5.3 collective-permute-start.70
  380.1 5.0 collective-permute-start.76
  408.6 5.4 collective-permute-start.79
  418.7 5.3 collective-permute-start.82
  435.6 5.0 collective-permute-start.88
  463.9 5.1 collective-permute-start.91
  473.7 5.3 collective-permute-start.94
  490.4 5.0 collective-permute-start.100
  518.9 5.2 collective-permute-start.103
  528.8 5.3 collective-permute-start.106
  545.7 5.0 collective-permute-start.112
  574.6 5.2 collective-permute-start.115
  584.5 5.3 collective-permute-start.118
  (96 other events, 382.0 us)
where the time goes:
time: 603 us; the launch traced here: 593 us
  other arithmetic  173 us (29%)
  starting transfers between devices  170 us (28%)
  waiting for transfers between devices  133 us (22%)
  local copies, waits for them, and re-layouts  114 us (19%)
    scatter-add x20, other arithmetic, spread(): buffer.at[:, head_atom].add(weighted).at[:, tail_atom].add(-weighted)  140 us
    ppermute x60, starting transfers between devices, with_halo(): after = lax.ppermute(leading, axis, down)  132 us
    ppermute x60, waiting for transfers between devices, with_halo(): before = lax.ppermute(last, axis, up)  92.8 us
    ppermute x60, waiting for transfers between devices, with_halo(): after = lax.ppermute(leading, axis, down)  40.5 us
    ppermute x60, starting transfers between devices, with_halo(): before = lax.ppermute(last, axis, up)  37.9 us
    gather x8, local copies, waits for them, and re-layouts, couple(): extended[:, head_atom] - extended[:, tail_atom]  32.1 us
    gather x8, local copies, waits for them, and re-layouts, couple(): extended[:, tail_atom]  27.3 us
    gather x2, local copies, waits for them, and re-layouts, per_device(): bond_scale = 1.0 / jnp.sqrt(ext_mass[0, head_atom] + ext_mass[0, tail_atom])  12.9 us
  transfers between devices with their start and end apart: 120, of which 98 were waited for; matrix products, arithmetic and copies ran while one was open for 0% of the time, Pallas kernels for 0%

commit v1 on v0

v1 whole, which is shorter than its diff:
```python
import functools

import jax
import jax.numpy as jnp
from jax import lax
from jax.experimental import pallas as pl
from jax.experimental.pallas import tpu as pltpu
from jax.sharding import PartitionSpec as P

MESH = pl.DeviceIdType.MESH
ATOMS = 1536
BONDS = 1024
SEND = 16
LANES = 128
AT = ATOMS // LANES
BT = BONDS // LANES
ST = 4
BLOCKS = [b for b in range(27) if b != 13]
ROW_OF = {b: n for n, b in enumerate(BLOCKS)}
F32 = jnp.float32
I32 = jnp.int32
PAIRS = [(0, 0), (0, 1), (0, 2), (1, 1), (1, 2), (2, 2)]


def take(rows, lane):
    numbers = lax.GatherDimensionNumbers(
        offset_dims=(),
        collapsed_slice_dims=(1,),
        start_index_map=(1,),
        operand_batching_dims=(0,),
        start_indices_batching_dims=(0,),
    )
    return lax.gather(
        rows, lane[..., None], numbers, (1, 1), mode=lax.GatherScatterMode.PROMISE_IN_BOUNDS
    )


def lookup(tiles, tile, lane):
    out = jnp.zeros(lane.shape, F32)
    for j, row in enumerate(tiles):
        out = jnp.where(tile == j, take(jnp.broadcast_to(row, lane.shape), lane), out)
    return out


def kernel(
    sizes,
    old_ref,
    move_ref,
    mass_ref,
    head_ref,
    tail_ref,
    send_ref,
    new_ref,
    mult_ref,
    table,
    idx,
    cols,
    incidence,
    coupling,
    inverse,
    vec,
    rows,
    sums,
    kinds,
    gathered,
    r0_out,
    a_out,
    a2_out,
    b_out,
    c_out,
    d_out,
    r0_in,
    a_in,
    a2_in,
    b_in,
    c_in,
    d_in,
    send_sem,
    recv_sem,
):
    names = ("gx", "gy", "gz")
    me = [lax.axis_index(n) for n in names]

    def device(block, sign):
        offs = (block // 9 - 1, block // 3 % 3 - 1, block % 3 - 1)
        return tuple(lax.rem(m + sign * o + n, n) for m, o, n in zip(me, offs, sizes))

    barrier = pltpu.get_barrier_semaphore()
    for b in BLOCKS:
        pl.semaphore_signal(barrier, inc=1, device_id=device(b, 1), device_id_type=MESH)

    def start(stage, source, target, sign):
        for b in BLOCKS:
            pltpu.make_async_remote_copy(
                src_ref=source(b),
                dst_ref=target.at[ROW_OF[b]],
                send_sem=send_sem.at[stage],
                recv_sem=recv_sem.at[stage],
                device_id=device(b, sign),
                device_id_type=MESH,
            ).start()

    def all_of(stage, target):
        return pltpu.make_async_remote_copy(
            src_ref=target,
            dst_ref=target,
            send_sem=send_sem.at[stage],
            recv_sem=recv_sem.at[stage],
            device_id=device(0, 1),
            device_id_type=MESH,
        )

    lane8 = lax.broadcasted_iota(I32, (8, LANES), 1)
    group8 = lane8 // SEND
    sub128 = lax.broadcasted_iota(I32, (LANES, LANES), 0)
    lane128 = lax.broadcasted_iota(I32, (LANES, LANES), 1)
    eye = sub128 == lane128

    for j in range(AT):
        cut = pl.ds(j * LANES, LANES)
        for i in range(3):
            table[j, i : i + 1, :] = old_ref[i, :, cut]
            table[j, 3 + i : 4 + i, :] = move_ref[i, :, cut]
        table[j, 6:7, :] = mass_ref[:, cut]
        table[j, 7:8, :] = jnp.zeros((1, LANES), F32)
    sent8 = jnp.broadcast_to(
        jnp.concatenate([send_ref[...]] * (LANES // SEND), axis=1), (8, LANES)
    )
    mine = jnp.zeros((8, LANES), F32)
    for j in range(AT):
        mine = jnp.where(sent8 // LANES == j, take(table[j], sent8 % LANES), mine)
    r0_out[...] = mine
    pl.semaphore_wait(barrier, len(BLOCKS))
    start(0, lambda b: r0_out, r0_in, -1)

    for t in range(BT):
        cut = pl.ds(t * LANES, LANES)
        idx[0, t : t + 1, :] = head_ref[:, cut]
        idx[1, t : t + 1, :] = tail_ref[:, cut]
    head = idx[0]
    tail = idx[1]
    is_halo = tail >= ATOMS
    slot = jnp.where(is_halo, tail - ATOMS, 0)
    near = jnp.where(is_halo, 0, tail)

    def at_ends(row):
        tiles = [row(j) for j in range(AT)]
        return (
            lookup(tiles, head // LANES, head % LANES),
            lookup(tiles, near // LANES, near % LANES),
        )

    ends = [at_ends(lambda j, k=k: table[j, k : k + 1, :]) for k in range(7)]
    head_mass = ends[6][0]
    near_mass = jnp.where(is_halo, 0.0, ends[6][1])

    def to_cols(k, value):
        for t in range(BT):
            col = jnp.sum(jnp.where(eye, value[t : t + 1, :], 0.0), axis=1, keepdims=True)
            cols[k, t * LANES : (t + 1) * LANES, :] = jnp.broadcast_to(col, (LANES, LANES))

    to_cols(0, head.astype(F32))
    to_cols(1, tail.astype(F32))
    to_cols(2, head_mass)
    to_cols(3, near_mass)

    inverse[...] = jnp.zeros((AT + ST, LANES), F32)

    def incidence_rows(t, carry):
        here = pl.ds(pl.multiple_of(t * LANES, LANES), LANES)
        heads = cols[0, here, :]
        tails = cols[1, here, :]
        number = (sub128 + (t * LANES + 1)).astype(F32)
        for j in range(AT + ST):
            atom = (lane128 + j * LANES).astype(F32)
            is_tail = tails == atom
            if j < AT:
                is_head = heads == atom
                incidence[here, j * LANES : (j + 1) * LANES] = (
                    jnp.where(is_head, 1.0, 0.0) - jnp.where(is_tail, 1.0, 0.0)
                ).astype(jnp.bfloat16)
                found = is_head
            else:
                found = is_tail
            inverse[j : j + 1, :] += jnp.sum(
                jnp.where(found, number, 0.0), axis=0, keepdims=True
            )
        return carry

    lax.fori_loop(0, BT, incidence_rows, 0)

    def merge(source, width):
        tiles = []
        for tile in range(ST):
            out = jnp.zeros((width, LANES), F32)
            for b in BLOCKS:
                if b // 8 == tile:
                    out = jnp.where(group8[:width] == b % 8, source[ROW_OF[b]], out)
            tiles.append(out)
        return tiles

    all_of(0, r0_in).wait_recv()
    halo = merge(r0_in, 8)
    slot_tile, slot_lane = slot // LANES, slot % LANES
    tail_data = []
    for k in range(7):
        far = lookup([halo[s][k : k + 1, :] for s in range(ST)], slot_tile, slot_lane)
        tail_data.append(jnp.where(is_halo, far, ends[k][1]))
    head_data = [e[0] for e in ends]

    bond = [head_data[i] - tail_data[i] for i in range(3)]
    length = jnp.maximum(jnp.sqrt(bond[0] * bond[0] + bond[1] * bond[1] + bond[2] * bond[2]), 0.5)
    direction = [b / length for b in bond]
    scale = 1.0 / jnp.sqrt(head_mass + tail_data[6])
    gain = [scale * d for d in direction]
    head_new = [head_data[i] + head_data[3 + i] for i in range(3)]
    tail_new = [tail_data[i] + tail_data[3 + i] for i in range(3)]
    shift = [head_new[i] - tail_new[i] for i in range(3)]
    right = scale * (
        direction[0] * shift[0] + direction[1] * shift[1] + direction[2] * shift[2] - length
    )
    own = 1.0 - head_mass * (gain[0] * gain[0] + gain[1] * gain[1] + gain[2] * gain[2])
    for i in range(3):
        to_cols(4 + i, gain[i])
    rows[0] = head.astype(F32)
    rows[1] = tail.astype(F32)
    for i in range(3):
        rows[2 + i] = gain[i]

    def coupling_rows(t, carry):
        here = pl.ds(pl.multiple_of(t * LANES, LANES), LANES)
        heads, tails = cols[0, here, :], cols[1, here, :]
        masses, near_masses = cols[2, here, :], cols[3, here, :]
        gains = [cols[4 + i, here, :] for i in range(3)]
        for u in range(BT):
            head_row, tail_row = rows[0, u : u + 1, :], rows[1, u : u + 1, :]
            shared = jnp.where(
                tails == head_row, -near_masses, jnp.where(tails == tail_row, near_masses, 0.0)
            ) - jnp.where(heads == tail_row, masses, 0.0)
            dots = (
                gains[0] * rows[2, u : u + 1, :]
                + gains[1] * rows[3, u : u + 1, :]
                + gains[2] * rows[4, u : u + 1, :]
            )
            coupling[here, u * LANES : (u + 1) * LANES] = shared * dots
        return carry

    lax.fori_loop(0, BT, coupling_rows, 0)

    def couple(values):
        for n, value in enumerate(values):
            vec[n] = value
        outs = [[] for _ in values]
        for t in range(BT):
            for n in range(len(values)):
                total = None
                for u in range(BT):
                    part = (
                        coupling[t * LANES : (t + 1) * LANES, u * LANES : (u + 1) * LANES]
                        * vec[n, u : u + 1, :]
                    )
                    total = part if total is None else total + part
                col = jnp.sum(total, axis=1, keepdims=True)
                outs[n].append(jnp.sum(jnp.where(eye, col, 0.0), axis=0, keepdims=True))
        return [own * v - jnp.concatenate(o, axis=0) for v, o in zip(values, outs)]

    def put_kinds(values):
        for k, value in enumerate(values):
            for t in range(BT):
                kinds[t, k : k + 1, :] = value[t : t + 1, :]

    slots = inverse[AT : AT + ST, :].astype(I32)

    def to_slots(values, out):
        width = out.shape[1]
        put_kinds(values)
        for s in range(ST):
            where = jnp.broadcast_to(slots[s : s + 1, :], (width, LANES))
            used = where > 0
            bond_of = jnp.maximum(where - 1, 0)
            tile, lane = bond_of // LANES, bond_of % LANES
            result = jnp.zeros((width, LANES), F32)
            for t in range(BT):
                result = jnp.where(tile == t, take(kinds[t, :width, :], lane), result)
            out[s] = jnp.where(used, result, 0.0)

    unit = jnp.where(is_halo, 1.0, 0.0)
    chain, reach = [right], [unit]
    for _ in range(3):
        nxt = couple([chain[-1], reach[-1]])
        chain.append(nxt[0])
        reach.append(nxt[1])
    zero = jnp.zeros((8, LANES), F32)
    to_slots(gain + reach[1:] + chain[0:2], a_out)
    start(1, lambda b: a_out.at[b // 8], a_in, 1)
    chain.append(couple([chain[-1]])[0])
    to_slots(chain[2:] + [zero], a2_out)
    start(2, lambda b: a2_out.at[b // 8], a2_in, 1)

    atom_bond = inverse[0:16, :].astype(I32)
    parent = lookup(
        [inverse[j : j + 1, :] for j in range(AT)], near // LANES, near % LANES
    ).astype(I32)
    has_parent = jnp.logical_and(parent > 0, jnp.logical_not(is_halo))
    parent = jnp.maximum(parent - 1, 0)
    root = jnp.where(is_halo, slot + 1, 0).astype(F32)
    label = root
    for _ in range(4):
        above = lookup([label[t : t + 1, :] for t in range(BT)], parent // LANES, parent % LANES)
        label = jnp.where(has_parent, above, root)
    bond_at = jnp.maximum(atom_bond - 1, 0)
    atom_label = lookup([label[t : t + 1, :] for t in range(BT)], bond_at // LANES, bond_at % LANES)
    row16 = lax.broadcasted_iota(I32, (16, LANES), 0)
    atom_label = jnp.where(
        jnp.logical_and(atom_bond > 0, row16 < AT), atom_label, 0.0
    ).astype(I32)
    label = label.astype(I32)

    def labelled(tiles, which):
        at = jnp.maximum(which - 1, 0)
        return jnp.where(which > 0, lookup(tiles, at // LANES, at % LANES), 0.0)

    def to_atoms(values):
        weighted = [v * g for v in values for g in gain]
        n = len(weighted)
        height = (n + 7) // 8 * 8
        put_kinds(weighted + [zero] * (height - n))
        full = jnp.concatenate([kinds[t, :height, :] for t in range(BT)], axis=1)
        high = full.astype(jnp.bfloat16)
        rest = full - high.astype(F32)
        mid = rest.astype(jnp.bfloat16)
        low = (rest - mid.astype(F32)).astype(jnp.bfloat16)
        total = None
        for part in (low, mid, high):
            product = jnp.dot(part, incidence[...], preferred_element_type=F32)
            total = product if total is None else total + product
        for j in range(AT):
            sums[j, :height, :] = total[:, j * LANES : (j + 1) * LANES]

    base = chain[0] + chain[1] + chain[2] + chain[3] + chain[4]
    grown = [reach[0]]
    for m in range(1, 4):
        grown.append(grown[-1] + reach[m])
    to_atoms([base] + grown)
    moves = []
    for n in range(15):
        at_head, at_near = at_ends(lambda j, n=n: sums[j, n : n + 1, :])
        moves.append(head_mass * at_head - near_mass * at_near)
    for n in range(15):
        for j in range(AT):
            gathered[n, j : j + 1, :] = sums[j, n : n + 1, :]
        gathered[n, AT:16, :] = jnp.zeros((16 - AT, LANES), F32)

    def by_kind(tiles, count):
        for s in range(ST):
            kinds[s, 0 : tiles[s].shape[0], :] = tiles[s]
        return [
            jnp.concatenate([kinds[s, k : k + 1, :] for s in range(ST)], axis=0)
            for k in range(count)
        ]

    def over_senders(values):
        lines = [jnp.sum(v, axis=0, keepdims=True) for v in values]
        lines += [jnp.zeros((1, LANES), F32)] * (-len(lines) % 8)
        block = jnp.concatenate(lines, axis=0)
        for step in (64, 32, 16):
            block = block + pltpu.roll(block, step, axis=1)
        return block

    own_mass = mine[6:7, :]

    def solve(sums_of, squares):
        found = []
        for k in range(5):
            now = []
            for i in range(3):
                total = sums_of(k, i)
                for j in range(k):
                    for m in range(3):
                        total = total + squares(k - 1 - j, i, m) * found[j][m]
                now.append(-own_mass * total)
            found.append(now)
        return found

    all_of(1, a_in).wait_recv()
    all_of(2, a2_in).wait_recv()
    first = by_kind(merge(a_in, 8), 8)
    second = by_kind(merge(a2_in, 4), 3)
    far_gain, far_reach, far_chain = first[0:3], first[3:6], first[6:8] + second
    lists = [far_gain[i] * far_chain[k] for k in range(5) for i in range(3)]
    squares_of = [far_gain[i] * far_gain[m] for i, m in PAIRS]
    lists += squares_of + [q * far_reach[n] for n in range(3) for q in squares_of]
    block = over_senders(lists)

    def squares(power, i, m):
        at = 15 + power * 6 + PAIRS.index((min(i, m), max(i, m)))
        return block[at : at + 1, :]

    found = solve(lambda k, i: block[3 * k + i : 3 * k + i + 1, :], squares)
    sent_total = [found[0][i] + found[1][i] + found[2][i] + found[3][i] + found[4][i] for i in range(3)]
    for k in range(4):
        z = sum(far_gain[i] * found[k][i] for i in range(3))
        for s in range(ST):
            b_out[s, k : k + 1, :] = z[s : s + 1, :]
    for i in range(3):
        moved = mine[i : i + 1, :] + mine[3 + i : 4 + i, :] - sent_total[i]
        for s in range(ST):
            b_out[s, 4 + i : 5 + i, :] = moved
    for s in range(ST):
        b_out[s, 7:8, :] = jnp.zeros((1, LANES), F32)
    start(3, lambda b: b_out.at[b // 8], b_in, -1)

    all_of(3, b_in).wait_recv()
    back = merge(b_in, 8)

    def kind_rows(tiles, k):
        return [tiles[s][k : k + 1, :] for s in range(ST)]

    z = [labelled(kind_rows(back, k), label) for k in range(4)]
    far_pos = [labelled(kind_rows(back, 4 + i), label) for i in range(3)]
    sol_one = base
    for j in range(4):
        sol_one = sol_one + z[j] * grown[3 - j]
    current = None
    for i in range(3):
        ahead = head_new[i] - jnp.where(is_halo, far_pos[i], tail_new[i])
        step = moves[i]
        for j in range(4):
            step = step + z[j] * moves[3 * (1 + 3 - j) + i]
        stretch = ahead - step
        current = stretch * stretch if current is None else current + stretch * stretch
    target = jnp.sqrt(jnp.maximum(2.0 * length * length - current, 0.5 * length * length))
    chain_two = [scale * (length - target)]
    for _ in range(4):
        chain_two.append(couple([chain_two[-1]])[0])
    to_slots(chain_two + [zero] * 3, c_out)
    start(4, lambda b: c_out.at[b // 8], c_in, 1)

    base_two = chain_two[0] + chain_two[1] + chain_two[2] + chain_two[3] + chain_two[4]
    to_atoms([base_two])
    mass_atoms = jnp.concatenate(
        [table[j, 6:7, :] for j in range(AT)] + [jnp.zeros((16 - AT, LANES), F32)], axis=0
    )
    still = []
    for i in range(3):
        spread_base = jnp.concatenate(
            [gathered[i, j : j + 1, :] + sums[j, i : i + 1, :] for j in range(AT)]
            + [jnp.zeros((16 - AT, LANES), F32)],
            axis=0,
        )
        start_pos = jnp.concatenate(
            [table[j, i : i + 1, :] + table[j, 3 + i : 4 + i, :] for j in range(AT)]
            + [jnp.zeros((16 - AT, LANES), F32)],
            axis=0,
        )
        still.append(start_pos - mass_atoms * spread_base)
    trees = [[mass_atoms * gathered[3 * (1 + n) + i] for i in range(3)] for n in range(4)]
    number16 = row16 * LANES + lax.broadcasted_iota(I32, (16, LANES), 1)
    which = jnp.zeros((16, LANES), I32)
    for e in range(SEND):
        which = jnp.where(number16 == sent8[0:1, e : e + 1], e + 1, which)

    all_of(4, c_in).wait_recv()
    far_two = by_kind(merge(c_in, 8), 5)
    block_two = over_senders([far_gain[i] * far_two[k] for k in range(5) for i in range(3)])
    found_two = solve(lambda k, i: block_two[3 * k + i : 3 * k + i + 1, :], squares)
    for k in range(4):
        z_two = sum(far_gain[i] * found_two[k][i] for i in range(3))
        for s in range(ST):
            d_out[s, k : k + 1, :] = z_two[s : s + 1, :]
    start(5, lambda b: d_out.at[b // 8], d_in, -1)

    for i in range(3):
        total = sent_total[i]
        for k in range(5):
            total = total + found_two[k][i]
        own_move = take(jnp.broadcast_to(total, (16, LANES)), jnp.maximum(which - 1, 0))
        still[i] = still[i] - jnp.where(which > 0, own_move, 0.0)

    all_of(5, d_in).wait_recv()
    last = merge(d_in, 4)
    result = sol_one + base_two
    for j in range(4):
        result = result + labelled(kind_rows(last, j), label) * grown[3 - j]
    for t in range(BT):
        mult_ref[:, t * LANES : (t + 1) * LANES] = result[t : t + 1, :]
    both = [[back[s][k : k + 1, :] + last[s][k : k + 1, :] for s in range(ST)] for k in range(4)]
    for j in range(4):
        z_atom = labelled(both[j], atom_label)
        for i in range(3):
            still[i] = still[i] - z_atom * trees[3 - j][i]
    for i in range(3):
        for j in range(AT):
            new_ref[i, :, j * LANES : (j + 1) * LANES] = still[i][j : j + 1, :]

    for stage, target in enumerate((r0_in, a_in, a2_in, b_in, c_in, d_in)):
        all_of(stage, target).wait_send()


def solution(mesh):
    sizes = tuple(mesh.shape[n] for n in ("gx", "gy", "gz"))

    def per_device(old_pos, displacement, inv_mass, bond_head, bond_tail, send_list):
        near = len(BLOCKS)
        vmem = pl.BlockSpec(memory_space=pltpu.VMEM)
        new_pos, multipliers = pl.pallas_call(
            functools.partial(kernel, sizes),
            out_shape=(
                jax.ShapeDtypeStruct((3, 1, ATOMS), F32),
                jax.ShapeDtypeStruct((1, BONDS), F32),
            ),
            in_specs=[vmem] * 6,
            out_specs=(vmem, vmem),
            scratch_shapes=[
                pltpu.VMEM((AT, 8, LANES), F32),
                pltpu.VMEM((2, 8, LANES), I32),
                pltpu.VMEM((7, BONDS, LANES), F32),
                pltpu.VMEM((BONDS, ATOMS), jnp.bfloat16),
                pltpu.VMEM((BONDS, BONDS), F32),
                pltpu.VMEM((AT + ST, LANES), F32),
                pltpu.VMEM((2, 8, LANES), F32),
                pltpu.VMEM((5, 8, LANES), F32),
                pltpu.VMEM((AT, 16, LANES), F32),
                pltpu.VMEM((8, 16, LANES), F32),
                pltpu.VMEM((15, 16, LANES), F32),
                pltpu.VMEM((8, LANES), F32),
                pltpu.VMEM((ST, 8, LANES), F32),
                pltpu.VMEM((ST, 4, LANES), F32),
                pltpu.VMEM((ST, 8, LANES), F32),
                pltpu.VMEM((ST, 8, LANES), F32),
                pltpu.VMEM((ST, 4, LANES), F32),
                pltpu.VMEM((near, 8, LANES), F32),
                pltpu.VMEM((near, 8, LANES), F32),
                pltpu.VMEM((near, 4, LANES), F32),
                pltpu.VMEM((near, 8, LANES), F32),
                pltpu.VMEM((near, 8, LANES), F32),
                pltpu.VMEM((near, 4, LANES), F32),
                pltpu.SemaphoreType.DMA((6,)),
                pltpu.SemaphoreType.DMA((6,)),
            ],
            compiler_params=pltpu.CompilerParams(collective_id=0, has_side_effects=True),
        )(
            old_pos.reshape(3, 1, ATOMS),
            displacement.reshape(3, 1, ATOMS),
            inv_mass.reshape(1, ATOMS),
            bond_head.reshape(1, BONDS),
            bond_tail.reshape(1, BONDS),
            send_list.reshape(1, SEND),
        )
        return new_pos.reshape(old_pos.shape), multipliers.reshape(bond_head.shape)

    return jax.shard_map(
        per_device,
        mesh=mesh,
        in_specs=(
            P(None, "gx", "gy", "gz", None),
            P(None, "gx", "gy", "gz", None),
            P("gx", "gy", "gz", None),
            P("gx", "gy", "gz", None),
            P("gx", "gy", "gz", None),
            P("gx", "gy", "gz", None),
        ),
        out_specs=(P(None, "gx", "gy", "gz", None), P("gx", "gy", "gz", None)),
        check_vma=False,
    )
```

time: 603 us -> 47.3 us (0.08)
  the two profiles are of different devices: /device:TPU:24 before, /device:TPU:1 now
where the time goes in v1:
time: 47.3 us; the launch traced here: 47.1 us
  Pallas kernels  44.6 us (94%)
  local copies, waits for them, and re-layouts  1.93 us (4%)
  between operations  0.65 us (1%)
    pallas_call x1, Pallas kernels, per_device(): pl.pallas_call(functools.partial(kernel, sizes), out_shape=(jax.ShapeDtyp...  44.6 us
    unnamed x4, local copies, waits for them, and re-layouts  1.93 us

profile of v1, /device:TPU:1, one launch (start us, length us, event | category | flops | bytes accessed | tf_op | source)
XLA Modules:
  0.0 47.1 jit_solution(9228319338217643078)
XLA Ops:
  0.6 44.6 %shard_map.77 = (f32[3,1,1536]{2,1,0:T(1,128)}, f32[1,1024]{1,0:T(1,128)}) custom-call(f32[3,1,1536]{2,1,0:T(1,128)} %bitcast.10, f32[3,1,1536]{2,1,0:T(1,128)} %bitcast.11, f32[1,1536]{1,0:T(1,128)} %bitcast.13, s32[1,1024]{1,0:T(1,128)} %bitcast.14, s32[1,1024]{1,0:T(1,128)} %bitcast.15, s32[1,16]{1,0:T(1,128)} %bitcast.17), custom_call_target="tpu_custom_call" | custom-call | tf_op jit(solution)/shard_map/pallas_call | solution.py:506
  45.2 0.0 copy-start
  45.2 1.3 %copy.11 = f32[3,1,1,1,1536]{4,3,2,1,0:T(1,128)} copy(f32[3,1,1,1,1536]{4,3,2,1,0:T(1,128)} %bitcast.12) | data formatting | bytes 36864
  46.5 0.0 copy-done
  46.5 0.6 %copy.12 = f32[1,1,1,1024]{3,2,1,0:T(1,128)} copy(f32[1,1,1,1024]{3,2,1,0:T(1,128)S(1)} %bitcast.16) | data formatting | bytes 8192
Async XLA Ops:
  45.2 1.3 %copy-start = (f32[1,1024]{1,0:T(1,128)S(1)}, f32[1,1024]{1,0:T(1,128)}, u32[]{:S(2)}) copy-start(f32[1,1024]{1,0:T(1,128)} %get-tuple-element.5) | copy-start | bytes 12292

commit v2 on v1

--- a/solution.py
+++ b/solution.py
@@ -56,6 +56,7 @@
     idx,
     cols,
     incidence,
+    trees_of,
     coupling,
     inverse,
     vec,
@@ -65,13 +66,11 @@
     gathered,
     r0_out,
     a_out,
-    a2_out,
     b_out,
     c_out,
     d_out,
     r0_in,
     a_in,
-    a2_in,
     b_in,
     c_in,
     d_in,
@@ -153,6 +152,8 @@
     ends = [at_ends(lambda j, k=k: table[j, k : k + 1, :]) for k in range(7)]
     head_mass = ends[6][0]
     near_mass = jnp.where(is_halo, 0.0, ends[6][1])
+    head_data = [e[0] for e in ends]
+    head_new = [head_data[i] + head_data[3 + i] for i in range(3)]
 
     def to_cols(k, value):
         for t in range(BT):
@@ -161,10 +162,33 @@
 
     to_cols(0, head.astype(F32))
     to_cols(1, tail.astype(F32))
-    to_cols(2, head_mass)
-    to_cols(3, near_mass)
+
+    def geometry(ahead, behind, mass, ahead_new, behind_new):
+        bond = [p - q for p, q in zip(ahead, behind)]
+        length = jnp.maximum(
+            jnp.sqrt(bond[0] * bond[0] + bond[1] * bond[1] + bond[2] * bond[2]), 0.5
+        )
+        direction = [b / length for b in bond]
+        scale = 1.0 / jnp.sqrt(mass)
+        shift = [p - q for p, q in zip(ahead_new, behind_new)]
+        right = scale * (
+            direction[0] * shift[0] + direction[1] * shift[1] + direction[2] * shift[2] - length
+        )
+        return length, scale, [scale * d for d in direction], right
+
+    near_data = [e[1] for e in ends]
+    _, _, tree_gain, tree_right = geometry(
+        head_data[0:3],
+        near_data[0:3],
+        head_mass + near_data[6],
+        head_new,
+        [near_data[i] + near_data[3 + i] for i in range(3)],
+    )
+    tree_gain = [jnp.where(is_halo, 0.0, g) for g in tree_gain]
+    tree_right = jnp.where(is_halo, 0.0, tree_right)
 
     inverse[...] = jnp.zeros((AT + ST, LANES), F32)
+    kinds[...] = jnp.zeros(kinds.shape, F32)
 
     def incidence_rows(t, carry):
         here = pl.ds(pl.multiple_of(t * LANES, LANES), LANES)
@@ -172,14 +196,13 @@
         tails = cols[1, here, :]
         number = (sub128 + (t * LANES + 1)).astype(F32)
         for j in range(AT + ST):
-            atom = (lane128 + j * LANES).astype(F32)
+            atom = (lane128[0:1] + j * LANES).astype(F32)
             is_tail = tails == atom
             if j < AT:
-                is_head = heads == atom
-                incidence[here, j * LANES : (j + 1) * LANES] = (
-                    jnp.where(is_head, 1.0, 0.0) - jnp.where(is_tail, 1.0, 0.0)
+                found = heads == atom
+                incidence[here, j * LANES : (j + 1) * LANES] = jnp.where(
+                    found, 1.0, jnp.where(is_tail, -1.0, 0.0)
                 ).astype(jnp.bfloat16)
-                found = is_head
             else:
                 found = is_tail
             inverse[j : j + 1, :] += jnp.sum(
@@ -189,13 +212,114 @@
 
     lax.fori_loop(0, BT, incidence_rows, 0)
 
-    def merge(source, width):
+    parent = lookup(
+        [inverse[j : j + 1, :] for j in range(AT)], near // LANES, near % LANES
+    ).astype(I32)
+    has_parent = jnp.logical_and(parent > 0, jnp.logical_not(is_halo))
+    parent = jnp.maximum(parent - 1, 0)
+    root = jnp.where(is_halo, slot + 1, 0).astype(F32)
+
+    def climb(label):
+        above = lookup([label[t : t + 1, :] for t in range(BT)], parent // LANES, parent % LANES)
+        return jnp.where(has_parent, above, root)
+
+    def put_kinds(values):
+        for k, value in enumerate(values):
+            for t in range(BT):
+                kinds[t, k : k + 1, :] = value[t : t + 1, :]
+
+    def times_ones(values, matrix):
+        height = (len(values) + 15) // 16 * 16
+        put_kinds(values)
+        full = jnp.concatenate([kinds[t, :height, :] for t in range(BT)], axis=1)
+        high = full.astype(jnp.bfloat16)
+        rest = full - high.astype(F32)
+        mid = rest.astype(jnp.bfloat16)
+        low = (rest - mid.astype(F32)).astype(jnp.bfloat16)
+        parts = jnp.concatenate([high, mid, low], axis=0)
+        product = jnp.dot(parts, matrix, preferred_element_type=F32)
+        return product[:height] + (product[height : 2 * height] + product[2 * height :])
+
+    def to_atoms(weighted):
+        total = times_ones(weighted, incidence[...])
+        height = (len(weighted) + 7) // 8 * 8
+        for j in range(AT):
+            sums[j, :height, :] = total[:height, j * LANES : (j + 1) * LANES]
+
+    def difference(n):
+        at_head, at_near = at_ends(lambda j: sums[j, n : n + 1, :])
+        return head_mass * at_head - near_mass * at_near
+
+    label_one = climb(root)
+    child = jnp.logical_and(label_one > 0.0, jnp.logical_not(is_halo))
+    label_two = climb(label_one)
+    start_of = [jnp.where(child, g, 0.0) for g in tree_gain]
+    to_atoms(
+        [tree_right * g for g in tree_gain]
+        + [start_of[i] * tree_gain[m] for i, m in PAIRS]
+    )
+    diffs = [difference(n) for n in range(9)]
+    tree_next = tree_right - sum(tree_gain[i] * diffs[i] for i in range(3))
+    start_next = []
+    for i in range(3):
+        start_next.append(
+            start_of[i]
+            - sum(
+                tree_gain[m] * diffs[3 + PAIRS.index((min(i, m), max(i, m)))] for m in range(3)
+            )
+        )
+    to_cols(2, label_two)
+    for s in range(ST):
+        number = (lane128[0:1] + (s * LANES + 1)).astype(F32)
+        trees_of[:, s * LANES : (s + 1) * LANES] = jnp.where(cols[2] == number, 1.0, 0.0).astype(
+            jnp.bfloat16
+        )
+    to_atoms([tree_next * g for g in tree_gain])
+    diffs = [difference(n) for n in range(3)]
+    tree_last = tree_next - sum(tree_gain[i] * diffs[i] for i in range(3))
+    tree_sums = times_ones(
+        [start_of[i] * start_of[m] for i, m in PAIRS]
+        + [start_of[i] * start_next[m] for i, m in PAIRS]
+        + [start_next[i] * start_next[m] for i, m in PAIRS]
+        + [y * tree_right for y in start_of]
+        + [y * tree_next for y in start_of]
+        + [y * tree_next for y in start_next]
+        + [y * tree_last for y in start_next],
+        trees_of[...],
+    )
+    slots = inverse[AT : AT + ST, :].astype(I32)
+    slot_bond = jnp.maximum(slots - 1, 0)
+    slot_head = lookup(
+        [head[t : t + 1, :].astype(F32) for t in range(BT)],
+        slot_bond // LANES,
+        slot_bond % LANES,
+    ).astype(I32)
+    for s in range(ST):
+        at = jnp.broadcast_to(slot_head[s : s + 1, :], (8, LANES))
+        used = jnp.broadcast_to(slots[s : s + 1, :], (8, LANES)) > 0
+        atoms = jnp.zeros((8, LANES), F32)
+        for j in range(AT):
+            atoms = jnp.where(at // LANES == j, take(table[j], at % LANES), atoms)
+        groups = [tree_sums[8 * n : 8 * n + 8, s * LANES : (s + 1) * LANES] for n in range(4)]
+        groups.append(jnp.where(used, atoms, 0.0))
+        turned = [pltpu.roll(g, SEND * n, axis=1) if n else g for n, g in enumerate(groups)]
+        for b in BLOCKS:
+            if b // 8 == s:
+                out = turned[0]
+                for n in range(1, len(turned)):
+                    out = jnp.where(group8 == (b + n) % 8, turned[n], out)
+                a_out[ROW_OF[b]] = out
+    start(1, lambda b: a_out.at[ROW_OF[b]], a_in, 1)
+
+    def merge(source, width, turn=0):
         tiles = []
         for tile in range(ST):
             out = jnp.zeros((width, LANES), F32)
             for b in BLOCKS:
                 if b // 8 == tile:
-                    out = jnp.where(group8[:width] == b % 8, source[ROW_OF[b]], out)
+                    out = jnp.where(group8[:width] == (b + turn) % 8, source[ROW_OF[b]], out)
+            if turn:
+                out = pltpu.roll(out, LANES - SEND * turn, axis=1)
             tiles.append(out)
         return tiles
 
@@ -205,21 +329,14 @@
     tail_data = []
     for k in range(7):
         far = lookup([halo[s][k : k + 1, :] for s in range(ST)], slot_tile, slot_lane)
-        tail_data.append(jnp.where(is_halo, far, ends[k][1]))
-    head_data = [e[0] for e in ends]
-
-    bond = [head_data[i] - tail_data[i] for i in range(3)]
-    length = jnp.maximum(jnp.sqrt(bond[0] * bond[0] + bond[1] * bond[1] + bond[2] * bond[2]), 0.5)
-    direction = [b / length for b in bond]
-    scale = 1.0 / jnp.sqrt(head_mass + tail_data[6])
-    gain = [scale * d for d in direction]
-    head_new = [head_data[i] + head_data[3 + i] for i in range(3)]
+        tail_data.append(jnp.where(is_halo, far, near_data[k]))
     tail_new = [tail_data[i] + tail_data[3 + i] for i in range(3)]
-    shift = [head_new[i] - tail_new[i] for i in range(3)]
-    right = scale * (
-        direction[0] * shift[0] + direction[1] * shift[1] + direction[2] * shift[2] - length
+    length, scale, gain, right = geometry(
+        head_data[0:3], tail_data[0:3], head_mass + tail_data[6], head_new, tail_new
     )
     own = 1.0 - head_mass * (gain[0] * gain[0] + gain[1] * gain[1] + gain[2] * gain[2])
+    to_cols(2, head_mass)
+    to_cols(3, near_mass)
     for i in range(3):
         to_cols(4 + i, gain[i])
     rows[0] = head.astype(F32)
@@ -264,93 +381,6 @@
                 outs[n].append(jnp.sum(jnp.where(eye, col, 0.0), axis=0, keepdims=True))
         return [own * v - jnp.concatenate(o, axis=0) for v, o in zip(values, outs)]
 
-    def put_kinds(values):
-        for k, value in enumerate(values):
-            for t in range(BT):
-                kinds[t, k : k + 1, :] = value[t : t + 1, :]
-
-    slots = inverse[AT : AT + ST, :].astype(I32)
-
-    def to_slots(values, out):
-        width = out.shape[1]
-        put_kinds(values)
-        for s in range(ST):
-            where = jnp.broadcast_to(slots[s : s + 1, :], (width, LANES))
-            used = where > 0
-            bond_of = jnp.maximum(where - 1, 0)
-            tile, lane = bond_of // LANES, bond_of % LANES
-            result = jnp.zeros((width, LANES), F32)
-            for t in range(BT):
-                result = jnp.where(tile == t, take(kinds[t, :width, :], lane), result)
-            out[s] = jnp.where(used, result, 0.0)
-
-    unit = jnp.where(is_halo, 1.0, 0.0)
-    chain, reach = [right], [unit]
-    for _ in range(3):
-        nxt = couple([chain[-1], reach[-1]])
-        chain.append(nxt[0])
-        reach.append(nxt[1])
-    zero = jnp.zeros((8, LANES), F32)
-    to_slots(gain + reach[1:] + chain[0:2], a_out)
-    start(1, lambda b: a_out.at[b // 8], a_in, 1)
-    chain.append(couple([chain[-1]])[0])
-    to_slots(chain[2:] + [zero], a2_out)
-    start(2, lambda b: a2_out.at[b // 8], a2_in, 1)
-
-    atom_bond = inverse[0:16, :].astype(I32)
-    parent = lookup(
-        [inverse[j : j + 1, :] for j in range(AT)], near // LANES, near % LANES
-    ).astype(I32)
-    has_parent = jnp.logical_and(parent > 0, jnp.logical_not(is_halo))
-    parent = jnp.maximum(parent - 1, 0)
-    root = jnp.where(is_halo, slot + 1, 0).astype(F32)
-    label = root
-    for _ in range(4):
-        above = lookup([label[t : t + 1, :] for t in range(BT)], parent // LANES, parent % LANES)
-        label = jnp.where(has_parent, above, root)
-    bond_at = jnp.maximum(atom_bond - 1, 0)
-    atom_label = lookup([label[t : t + 1, :] for t in range(BT)], bond_at // LANES, bond_at % LANES)
-    row16 = lax.broadcasted_iota(I32, (16, LANES), 0)
-    atom_label = jnp.where(
-        jnp.logical_and(atom_bond > 0, row16 < AT), atom_label, 0.0
-    ).astype(I32)
-    label = label.astype(I32)
-
-    def labelled(tiles, which):
-        at = jnp.maximum(which - 1, 0)
-        return jnp.where(which > 0, lookup(tiles, at // LANES, at % LANES), 0.0)
-
-    def to_atoms(values):
-        weighted = [v * g for v in values for g in gain]
-        n = len(weighted)
-        height = (n + 7) // 8 * 8
-        put_kinds(weighted + [zero] * (height - n))
-        full = jnp.concatenate([kinds[t, :height, :] for t in range(BT)], axis=1)
-        high = full.astype(jnp.bfloat16)
-        rest = full - high.astype(F32)
-        mid = rest.astype(jnp.bfloat16)
-        low = (rest - mid.astype(F32)).astype(jnp.bfloat16)
-        total = None
-        for part in (low, mid, high):
-            product = jnp.dot(part, incidence[...], preferred_element_type=F32)
-            total = product if total is None else total + product
-        for j in range(AT):
-            sums[j, :height, :] = total[:, j * LANES : (j + 1) * LANES]
-
-    base = chain[0] + chain[1] + chain[2] + chain[3] + chain[4]
-    grown = [reach[0]]
-    for m in range(1, 4):
-        grown.append(grown[-1] + reach[m])
-    to_atoms([base] + grown)
-    moves = []
-    for n in range(15):
-        at_head, at_near = at_ends(lambda j, n=n: sums[j, n : n + 1, :])
-        moves.append(head_mass * at_head - near_mass * at_near)
-    for n in range(15):
-        for j in range(AT):
-            gathered[n, j : j + 1, :] = sums[j, n : n + 1, :]
-        gathered[n, AT:16, :] = jnp.zeros((16 - AT, LANES), F32)
-
     def by_kind(tiles, count):
         for s in range(ST):
             kinds[s, 0 : tiles[s].shape[0], :] = tiles[s]
@@ -383,10 +413,42 @@
         return found
 
     all_of(1, a_in).wait_recv()
-    all_of(2, a2_in).wait_recv()
-    first = by_kind(merge(a_in, 8), 8)
-    second = by_kind(merge(a2_in, 4), 3)
-    far_gain, far_reach, far_chain = first[0:3], first[3:6], first[6:8] + second
+    far = []
+    for n in range(5):
+        far += by_kind(merge(a_in, 8, n), 8)
+    far_head, far_mass = far[32:38], far[38]
+    far_new = [far_head[i] + far_head[3 + i] for i in range(3)]
+    used = far_mass > 0.0
+    _, _, far_gain, far_right = geometry(
+        far_head[0:3],
+        [mine[i : i + 1, :] for i in range(3)],
+        far_mass + own_mass,
+        far_new,
+        [mine[i : i + 1, :] + mine[3 + i : 4 + i, :] for i in range(3)],
+    )
+    far_gain = [jnp.where(used, g, 0.0) for g in far_gain]
+    far_right = jnp.where(used, far_right, 0.0)
+    pull = [far_mass * g for g in far_gain]
+    far_own = 1.0 - (pull[0] * far_gain[0] + pull[1] * far_gain[1] + pull[2] * far_gain[2])
+    turn = []
+    for power in range(3):
+        form = far[6 * power : 6 * power + 6]
+        turn.append(
+            sum(
+                pull[i] * sum(pull[m] * form[PAIRS.index((min(i, m), max(i, m)))] for m in range(3))
+                for i in range(3)
+            )
+        )
+    feed = [sum(pull[i] * far[18 + 3 * k + i] for i in range(3)) for k in range(4)]
+    far_chain = [far_right]
+    for k in range(4):
+        value = far_own * far_chain[k] + feed[k]
+        for j in range(k):
+            value = value + turn[k - 1 - j] * far_chain[j]
+        far_chain.append(value)
+    far_reach = [far_own]
+    far_reach.append(far_own * far_own + turn[0])
+    far_reach.append(far_own * far_reach[1] + turn[0] * far_own + turn[1])
     lists = [far_gain[i] * far_chain[k] for k in range(5) for i in range(3)]
     squares_of = [far_gain[i] * far_gain[m] for i, m in PAIRS]
     lists += squares_of + [q * far_reach[n] for n in range(3) for q in squares_of]
@@ -409,6 +471,41 @@
     for s in range(ST):
         b_out[s, 7:8, :] = jnp.zeros((1, LANES), F32)
     start(3, lambda b: b_out.at[b // 8], b_in, -1)
+
+
+    label = climb(climb(label_two))
+    atom_bond = inverse[0:16, :].astype(I32)
+    bond_at = jnp.maximum(atom_bond - 1, 0)
+    atom_label = lookup([label[t : t + 1, :] for t in range(BT)], bond_at // LANES, bond_at % LANES)
+    row16 = lax.broadcasted_iota(I32, (16, LANES), 0)
+    atom_label = jnp.where(
+        jnp.logical_and(atom_bond > 0, row16 < AT), atom_label, 0.0
+    ).astype(I32)
+    label = label.astype(I32)
+
+    def labelled(tiles, which):
+        at = jnp.maximum(which - 1, 0)
+        return jnp.where(which > 0, lookup(tiles, at // LANES, at % LANES), 0.0)
+
+    unit = jnp.where(is_halo, 1.0, 0.0)
+    chain, reach = [right], [unit]
+    for _ in range(3):
+        nxt = couple([chain[-1], reach[-1]])
+        chain.append(nxt[0])
+        reach.append(nxt[1])
+    chain.append(couple([chain[-1]])[0])
+    base = chain[0] + chain[1] + chain[2] + chain[3] + chain[4]
+    grown = [reach[0]]
+    for m in range(1, 4):
+        grown.append(grown[-1] + reach[m])
+    to_atoms([v * g for v in [base] + grown for g in gain])
+    moves = []
+    for n in range(15):
+        moves.append(difference(n))
+    for n in range(15):
+        for j in range(AT):
+            gathered[n, j : j + 1, :] = sums[j, n : n + 1, :]
+        gathered[n, AT:16, :] = jnp.zeros((16 - AT, LANES), F32)
 
     all_of(3, b_in).wait_recv()
     back = merge(b_in, 8)
@@ -431,13 +528,20 @@
         current = stretch * stretch if current is None else current + stretch * stretch
     target = jnp.sqrt(jnp.maximum(2.0 * length * length - current, 0.5 * length * length))
     chain_two = [scale * (length - target)]
-    for _ in range(4):
+    for _ in range(2):
         chain_two.append(couple([chain_two[-1]])[0])
-    to_slots(chain_two + [zero] * 3, c_out)
+    tree_sums = times_ones(
+        [unit * v for v in chain_two] + [reach[1] * chain_two[2], reach[2] * chain_two[2]],
+        trees_of[...],
+    )
+    for s in range(ST):
+        c_out[s] = tree_sums[0:8, s * LANES : (s + 1) * LANES]
     start(4, lambda b: c_out.at[b // 8], c_in, 1)
+    for _ in range(2):
+        chain_two.append(couple([chain_two[-1]])[0])
 
     base_two = chain_two[0] + chain_two[1] + chain_two[2] + chain_two[3] + chain_two[4]
-    to_atoms([base_two])
+    to_atoms([base_two * g for g in gain])
     mass_atoms = jnp.concatenate(
         [table[j, 6:7, :] for j in range(AT)] + [jnp.zeros((16 - AT, LANES), F32)], axis=0
     )
@@ -493,7 +597,7 @@
         for j in range(AT):
             new_ref[i, :, j * LANES : (j + 1) * LANES] = still[i][j : j + 1, :]
 
-    for stage, target in enumerate((r0_in, a_in, a2_in, b_in, c_in, d_in)):
+    for stage, target in ((0, r0_in), (1, a_in), (3, b_in), (4, c_in), (5, d_in)):
         all_of(stage, target).wait_send()
 
 
@@ -516,22 +620,21 @@
                 pltpu.VMEM((2, 8, LANES), I32),
                 pltpu.VMEM((7, BONDS, LANES), F32),
                 pltpu.VMEM((BONDS, ATOMS), jnp.bfloat16),
+                pltpu.VMEM((BONDS, ST * LANES), jnp.bfloat16),
                 pltpu.VMEM((BONDS, BONDS), F32),
                 pltpu.VMEM((AT + ST, LANES), F32),
                 pltpu.VMEM((2, 8, LANES), F32),
                 pltpu.VMEM((5, 8, LANES), F32),
                 pltpu.VMEM((AT, 16, LANES), F32),
-                pltpu.VMEM((8, 16, LANES), F32),
+                pltpu.VMEM((8, 40, LANES), F32),
                 pltpu.VMEM((15, 16, LANES), F32),
                 pltpu.VMEM((8, LANES), F32),
-                pltpu.VMEM((ST, 8, LANES), F32),
-                pltpu.VMEM((ST, 4, LANES), F32),
+                pltpu.VMEM((near, 8, LANES), F32),
                 pltpu.VMEM((ST, 8, LANES), F32),
                 pltpu.VMEM((ST, 8, LANES), F32),
                 pltpu.VMEM((ST, 4, LANES), F32),
                 pltpu.VMEM((near, 8, LANES), F32),
                 pltpu.VMEM((near, 8, LANES), F32),
-                pltpu.VMEM((near, 4, LANES), F32),
                 pltpu.VMEM((near, 8, LANES), F32),
                 pltpu.VMEM((near, 8, LANES), F32),
                 pltpu.VMEM((near, 4, LANES), F32),

time: 47.3 us -> 40.9 us (0.86)
  Pallas kernels: 44.6 us -> 38.2 us
    pallas_call x1, Pallas kernels: 44.6 us -> 38.2 us  [per_device(): pl.pallas_call(functools.partial(kernel, sizes), out_shape=(jax.ShapeDtyp...]
where the time goes in v2:
time: 40.9 us; the launch traced here: 40.8 us
  Pallas kernels  38.2 us (93%)
  local copies, waits for them, and re-layouts  1.93 us (5%)
  between operations  0.65 us (2%)
    pallas_call x1, Pallas kernels, per_device(): pl.pallas_call(functools.partial(kernel, sizes), out_shape=(jax.ShapeDtyp...  38.2 us
    unnamed x4, local copies, waits for them, and re-layouts  1.93 us

profile of v2, /device:TPU:1, one launch (start us, length us, event | category | flops | bytes accessed | tf_op | source)
XLA Modules:
  0.0 40.8 jit_solution(17649412876210859413)
XLA Ops:
  0.6 38.2 %shard_map.77 = (f32[3,1,1536]{2,1,0:T(1,128)}, f32[1,1024]{1,0:T(1,128)}) custom-call(f32[3,1,1536]{2,1,0:T(1,128)} %bitcast.10, f32[3,1,1536]{2,1,0:T(1,128)} %bitcast.11, f32[1,1536]{1,0:T(1,128)} %bitcast.13, s32[1,1024]{1,0:T(1,128)} %bitcast.14, s32[1,1024]{1,0:T(1,128)} %bitcast.15, s32[1,16]{1,0:T(1,128)} %bitcast.17), custom_call_target="tpu_custom_call" | custom-call | tf_op jit(solution)/shard_map/pallas_call | solution.py:610
  38.8 0.0 copy-start
  38.8 1.3 %copy.11 = f32[3,1,1,1,1536]{4,3,2,1,0:T(1,128)} copy(f32[3,1,1,1,1536]{4,3,2,1,0:T(1,128)} %bitcast.12) | data formatting | bytes 36864
  40.2 0.0 copy-done
  40.2 0.6 %copy.12 = f32[1,1,1,1024]{3,2,1,0:T(1,128)} copy(f32[1,1,1,1024]{3,2,1,0:T(1,128)S(1)} %bitcast.16) | data formatting | bytes 8192
Async XLA Ops:
  38.8 1.3 %copy-start = (f32[1,1024]{1,0:T(1,128)S(1)}, f32[1,1024]{1,0:T(1,128)}, u32[]{:S(2)}) copy-start(f32[1,1024]{1,0:T(1,128)} %get-tuple-element.5) | copy-start | bytes 12292

commit v3 on v2

--- a/solution.py
+++ b/solution.py
@@ -44,20 +44,28 @@
 
 def kernel(
     sizes,
+    old_hbm,
+    move_hbm,
+    mass_hbm,
+    head_hbm,
+    tail_hbm,
+    send_hbm,
+    new_ref,
+    mult_ref,
     old_ref,
     move_ref,
     mass_ref,
     head_ref,
     tail_ref,
     send_ref,
-    new_ref,
-    mult_ref,
+    load_sem,
     table,
     idx,
     cols,
     incidence,
     trees_of,
     coupling,
+    found_by,
     inverse,
     vec,
     rows,
@@ -77,6 +85,21 @@
     send_sem,
     recv_sem,
 ):
+    loads = [
+        pltpu.make_async_copy(source, target, load_sem.at[n])
+        for n, (source, target) in enumerate(
+            (
+                (send_hbm, send_ref),
+                (old_hbm, old_ref),
+                (move_hbm, move_ref),
+                (mass_hbm, mass_ref),
+                (head_hbm, head_ref),
+                (tail_hbm, tail_ref),
+            )
+        )
+    ]
+    for load in loads:
+        load.start()
     names = ("gx", "gy", "gz")
     me = [lax.axis_index(n) for n in names]
 
@@ -115,6 +138,8 @@
     lane128 = lax.broadcasted_iota(I32, (LANES, LANES), 1)
     eye = sub128 == lane128
 
+    for load in loads:
+        load.wait()
     for j in range(AT):
         cut = pl.ds(j * LANES, LANES)
         for i in range(3):
@@ -129,8 +154,6 @@
     for j in range(AT):
         mine = jnp.where(sent8 // LANES == j, take(table[j], sent8 % LANES), mine)
     r0_out[...] = mine
-    pl.semaphore_wait(barrier, len(BLOCKS))
-    start(0, lambda b: r0_out, r0_in, -1)
 
     for t in range(BT):
         cut = pl.ds(t * LANES, LANES)
@@ -187,7 +210,7 @@
     tree_gain = [jnp.where(is_halo, 0.0, g) for g in tree_gain]
     tree_right = jnp.where(is_halo, 0.0, tree_right)
 
-    inverse[...] = jnp.zeros((AT + ST, LANES), F32)
+    found_by[...] = jnp.zeros(found_by.shape, F32)
     kinds[...] = jnp.zeros(kinds.shape, F32)
 
     def incidence_rows(t, carry):
@@ -195,22 +218,33 @@
         heads = cols[0, here, :]
         tails = cols[1, here, :]
         number = (sub128 + (t * LANES + 1)).astype(F32)
+        cuts = [slice(8 * r, 8 * r + 8) for r in range(LANES // 8)]
         for j in range(AT + ST):
-            atom = (lane128[0:1] + j * LANES).astype(F32)
-            is_tail = tails == atom
+            atom = (lane8 + j * LANES).astype(F32)
+            number_of = found_by[j]
+            parts = []
+            for cut in cuts:
+                if j < AT:
+                    found = heads[cut] == atom
+                    parts.append(
+                        jnp.where(found, 1.0, jnp.where(tails[cut] == atom, -1.0, 0.0))
+                    )
+                else:
+                    found = tails[cut] == atom
+                number_of = jnp.where(found, number[cut], number_of)
+            found_by[j] = number_of
             if j < AT:
-                found = heads == atom
-                incidence[here, j * LANES : (j + 1) * LANES] = jnp.where(
-                    found, 1.0, jnp.where(is_tail, -1.0, 0.0)
+                incidence[here, j * LANES : (j + 1) * LANES] = jnp.concatenate(
+                    parts, axis=0
                 ).astype(jnp.bfloat16)
-            else:
-                found = is_tail
-            inverse[j : j + 1, :] += jnp.sum(
-                jnp.where(found, number, 0.0), axis=0, keepdims=True
-            )
         return carry
 
-    lax.fori_loop(0, BT, incidence_rows, 0)
+    lax.fori_loop(0, 2, incidence_rows, 0)
+    pl.semaphore_wait(barrier, len(BLOCKS))
+    start(0, lambda b: r0_out, r0_in, -1)
+    lax.fori_loop(2, BT, incidence_rows, 0)
+    for j in range(AT + ST):
+        inverse[j : j + 1, :] = jnp.sum(found_by[j], axis=0, keepdims=True)
 
     parent = lookup(
         [inverse[j : j + 1, :] for j in range(AT)], near // LANES, near % LANES
@@ -595,10 +629,16 @@
             still[i] = still[i] - z_atom * trees[3 - j][i]
     for i in range(3):
         for j in range(AT):
-            new_ref[i, :, j * LANES : (j + 1) * LANES] = still[i][j : j + 1, :]
+            at = i * ATOMS + j * LANES
+            new_ref[:, at : at + LANES] = still[i][j : j + 1, :]
 
     for stage, target in ((0, r0_in), (1, a_in), (3, b_in), (4, c_in), (5, d_in)):
         all_of(stage, target).wait_send()
+
+
+def write_out(new_ref, mult_ref, new_out, mult_out):
+    new_out[...] = new_ref[...]
+    mult_out[...] = mult_ref[...]
 
 
 def solution(mesh):
@@ -609,19 +649,24 @@
         vmem = pl.BlockSpec(memory_space=pltpu.VMEM)
         new_pos, multipliers = pl.pallas_call(
             functools.partial(kernel, sizes),
-            out_shape=(
-                jax.ShapeDtypeStruct((3, 1, ATOMS), F32),
-                jax.ShapeDtypeStruct((1, BONDS), F32),
-            ),
-            in_specs=[vmem] * 6,
+            out_shape=(pltpu.VMEM((1, 3 * ATOMS), F32), pltpu.VMEM((1, BONDS), F32)),
+            in_specs=[pl.BlockSpec(memory_space=pl.ANY)] * 6,
             out_specs=(vmem, vmem),
             scratch_shapes=[
+                pltpu.VMEM((3, 1, ATOMS), F32),
+                pltpu.VMEM((3, 1, ATOMS), F32),
+                pltpu.VMEM((1, ATOMS), F32),
+                pltpu.VMEM((1, BONDS), I32),
+                pltpu.VMEM((1, BONDS), I32),
+                pltpu.VMEM((1, SEND), I32),
+                pltpu.SemaphoreType.DMA((6,)),
                 pltpu.VMEM((AT, 8, LANES), F32),
                 pltpu.VMEM((2, 8, LANES), I32),
                 pltpu.VMEM((7, BONDS, LANES), F32),
                 pltpu.VMEM((BONDS, ATOMS), jnp.bfloat16),
                 pltpu.VMEM((BONDS, ST * LANES), jnp.bfloat16),
                 pltpu.VMEM((BONDS, BONDS), F32),
+                pltpu.VMEM((AT + ST, 8, LANES), F32),
                 pltpu.VMEM((AT + ST, LANES), F32),
                 pltpu.VMEM((2, 8, LANES), F32),
                 pltpu.VMEM((5, 8, LANES), F32),
@@ -650,6 +695,18 @@
             bond_tail.reshape(1, BONDS),
             send_list.reshape(1, SEND),
         )
+        new_pos, multipliers = pl.pallas_call(
+            write_out,
+            out_shape=(
+                jax.ShapeDtypeStruct((1, 3 * ATOMS), F32),
+                jax.ShapeDtypeStruct((1, BONDS), F32),
+            ),
+            in_specs=[vmem] * 2,
+            out_specs=(vmem, vmem),
+        )(
+            pltpu.with_memory_space_constraint(new_pos, pltpu.VMEM),
+            pltpu.with_memory_space_constraint(multipliers, pltpu.VMEM),
+        )
         return new_pos.reshape(old_pos.shape), multipliers.reshape(bond_head.shape)
 
     return jax.shard_map(

time: 40.9 us -> 37.2 us (0.910)
  local copies, waits for them, and re-layouts: 1.93 us -> 0 us
  Pallas kernels: 38.2 us -> 36.4 us
    unnamed x4 -> x0, local copies, waits for them, and re-layouts: 1.93 us -> none
    pallas_call x1 -> x2, Pallas kernels: 38.2 us -> 36.4 us  [the longest x1 35.8 us: per_device(): pl.pallas_call(functools.partial(kernel, sizes), out_shape=(pltpu.VMEM((1...]
where the time goes in v3:
time: 37.2 us; the launch traced here: 37.1 us
  Pallas kernels  36.4 us (98%)
  between operations  0.64 us (2%)
    pallas_call x1, Pallas kernels, per_device(): pl.pallas_call(functools.partial(kernel, sizes), out_shape=(pltpu.VMEM((1...  35.8 us

profile of v3, /device:TPU:1, one launch (start us, length us, event | category | flops | bytes accessed | tf_op | source)
XLA Modules:
  0.0 37.1 jit_solution(11161460698147344751)
XLA Ops:
  0.6 35.8 %shard_map.77 = (f32[1,4608]{1,0:T(1,128)S(1)}, f32[1,1024]{1,0:T(1,128)S(1)}) custom-call(f32[3,1,1536]{2,1,0:T(1,128)} %bitcast.8, f32[3,1,1536]{2,1,0:T(1,128)} %bitcast.9, f32[1,1536]{1,0:T(1,128)} %bitcast.10, s32[1,1024]{1,0:T(1,128)} %bitcast.11, s32[1,1024]{1,0:T(1,128)} %bitcast.12, s32[1,16]{1,0:T(1,128)} %bitcast.13), custom_call_target="tpu_custom_call" | custom-call | tf_op jit(solution)/shard_map/pallas_call | solution.py:650
  36.4 0.6 %shard_map.78 = (f32[1,4608]{1,0:T(1,128)}, f32[1,1024]{1,0:T(1,128)}) custom-call(f32[1,4608]{1,0:T(1,128)S(1)} %get-tuple-element.6.new_ref, f32[1,1024]{1,0:T(1,128)S(1)} %get-tuple-element.7.mult_ref), custom_call_target="tpu_custom_call" | custom-call | tf_op jit(solution)/shard_map/pallas_call | solution.py:698

commit v4 on v3

--- a/solution.py
+++ b/solution.py
@@ -74,11 +74,13 @@
     gathered,
     r0_out,
     a_out,
+    a2_out,
     b_out,
     c_out,
     d_out,
     r0_in,
     a_in,
+    a2_in,
     b_in,
     c_in,
     d_in,
@@ -302,23 +304,20 @@
                 tree_gain[m] * diffs[3 + PAIRS.index((min(i, m), max(i, m)))] for m in range(3)
             )
         )
-    to_cols(2, label_two)
+    label = climb(climb(label_two))
+    to_cols(7, label)
     for s in range(ST):
         number = (lane128[0:1] + (s * LANES + 1)).astype(F32)
-        trees_of[:, s * LANES : (s + 1) * LANES] = jnp.where(cols[2] == number, 1.0, 0.0).astype(
+        trees_of[:, s * LANES : (s + 1) * LANES] = jnp.where(cols[7] == number, 1.0, 0.0).astype(
             jnp.bfloat16
         )
-    to_atoms([tree_next * g for g in tree_gain])
-    diffs = [difference(n) for n in range(3)]
-    tree_last = tree_next - sum(tree_gain[i] * diffs[i] for i in range(3))
     tree_sums = times_ones(
         [start_of[i] * start_of[m] for i, m in PAIRS]
         + [start_of[i] * start_next[m] for i, m in PAIRS]
         + [start_next[i] * start_next[m] for i, m in PAIRS]
         + [y * tree_right for y in start_of]
         + [y * tree_next for y in start_of]
-        + [y * tree_next for y in start_next]
-        + [y * tree_last for y in start_next],
+        + [y * tree_next for y in start_next],
         trees_of[...],
     )
     slots = inverse[AT : AT + ST, :].astype(I32)
@@ -344,6 +343,13 @@
                     out = jnp.where(group8 == (b + n) % 8, turned[n], out)
                 a_out[ROW_OF[b]] = out
     start(1, lambda b: a_out.at[ROW_OF[b]], a_in, 1)
+    to_atoms([tree_next * g for g in tree_gain])
+    diffs = [difference(n) for n in range(3)]
+    tree_last = tree_next - sum(tree_gain[i] * diffs[i] for i in range(3))
+    tree_sums = times_ones([y * tree_last for y in start_next], trees_of[...])
+    for s in range(ST):
+        a2_out[s] = tree_sums[0:4, s * LANES : (s + 1) * LANES]
+    start(2, lambda b: a2_out.at[b // 8], a2_in, 1)
 
     def merge(source, width, turn=0):
         tiles = []
@@ -357,6 +363,10 @@
             tiles.append(out)
         return tiles
 
+    to_cols(2, head_mass)
+    to_cols(3, near_mass)
+    rows[0] = head.astype(F32)
+    rows[1] = tail.astype(F32)
     all_of(0, r0_in).wait_recv()
     halo = merge(r0_in, 8)
     slot_tile, slot_lane = slot // LANES, slot % LANES
@@ -369,34 +379,32 @@
         head_data[0:3], tail_data[0:3], head_mass + tail_data[6], head_new, tail_new
     )
     own = 1.0 - head_mass * (gain[0] * gain[0] + gain[1] * gain[1] + gain[2] * gain[2])
-    to_cols(2, head_mass)
-    to_cols(3, near_mass)
     for i in range(3):
         to_cols(4 + i, gain[i])
-    rows[0] = head.astype(F32)
-    rows[1] = tail.astype(F32)
     for i in range(3):
         rows[2 + i] = gain[i]
 
     def coupling_rows(t, carry):
-        here = pl.ds(pl.multiple_of(t * LANES, LANES), LANES)
-        heads, tails = cols[0, here, :], cols[1, here, :]
-        masses, near_masses = cols[2, here, :], cols[3, here, :]
-        gains = [cols[4 + i, here, :] for i in range(3)]
-        for u in range(BT):
-            head_row, tail_row = rows[0, u : u + 1, :], rows[1, u : u + 1, :]
-            shared = jnp.where(
-                tails == head_row, -near_masses, jnp.where(tails == tail_row, near_masses, 0.0)
-            ) - jnp.where(heads == tail_row, masses, 0.0)
-            dots = (
-                gains[0] * rows[2, u : u + 1, :]
-                + gains[1] * rows[3, u : u + 1, :]
-                + gains[2] * rows[4, u : u + 1, :]
-            )
-            coupling[here, u * LANES : (u + 1) * LANES] = shared * dots
+        for part in range(2):
+            here = pl.ds(pl.multiple_of(t * 64 + part * 32, 32), 32)
+            heads, tails = cols[0, here, :], cols[1, here, :]
+            masses, near_masses = cols[2, here, :], cols[3, here, :]
+            minus_near = -near_masses
+            gains = [cols[4 + i, here, :] for i in range(3)]
+            for u in range(BT):
+                head_row, tail_row = rows[0, u : u + 1, :], rows[1, u : u + 1, :]
+                shared = jnp.where(
+                    tails == head_row, minus_near, jnp.where(tails == tail_row, near_masses, 0.0)
+                ) - jnp.where(heads == tail_row, masses, 0.0)
+                dots = (
+                    gains[0] * rows[2, u : u + 1, :]
+                    + gains[1] * rows[3, u : u + 1, :]
+                    + gains[2] * rows[4, u : u + 1, :]
+                )
+                coupling[here, u * LANES : (u + 1) * LANES] = shared * dots
         return carry
 
-    lax.fori_loop(0, BT, coupling_rows, 0)
+    lax.fori_loop(0, BONDS // 64, coupling_rows, 0)
 
     def couple(values):
         for n, value in enumerate(values):
@@ -427,15 +435,15 @@
         lines = [jnp.sum(v, axis=0, keepdims=True) for v in values]
         lines += [jnp.zeros((1, LANES), F32)] * (-len(lines) % 8)
         block = jnp.concatenate(lines, axis=0)
-        for step in (64, 32, 16):
-            block = block + pltpu.roll(block, step, axis=1)
-        return block
+        turned = [pltpu.roll(block, SEND * n, axis=1) for n in range(1, LANES // SEND)]
+        return ((block + turned[0]) + (turned[1] + turned[2])) + (
+            (turned[3] + turned[4]) + (turned[5] + turned[6])
+        )
 
     own_mass = mine[6:7, :]
 
-    def solve(sums_of, squares):
-        found = []
-        for k in range(5):
+    def solve(sums_of, squares, found, count):
+        for k in range(len(found), count):
             now = []
             for i in range(3):
                 total = sums_of(k, i)
@@ -453,7 +461,7 @@
     far_head, far_mass = far[32:38], far[38]
     far_new = [far_head[i] + far_head[3 + i] for i in range(3)]
     used = far_mass > 0.0
-    _, _, far_gain, far_right = geometry(
+    far_length, far_scale, far_gain, far_right = geometry(
         far_head[0:3],
         [mine[i : i + 1, :] for i in range(3)],
         far_mass + own_mass,
@@ -473,41 +481,38 @@
                 for i in range(3)
             )
         )
-    feed = [sum(pull[i] * far[18 + 3 * k + i] for i in range(3)) for k in range(4)]
+    feed = [sum(pull[i] * far[18 + 3 * k + i] for i in range(3)) for k in range(3)]
     far_chain = [far_right]
-    for k in range(4):
+
+    def next_chain():
+        k = len(far_chain) - 1
         value = far_own * far_chain[k] + feed[k]
         for j in range(k):
             value = value + turn[k - 1 - j] * far_chain[j]
         far_chain.append(value)
+
+    for _ in range(3):
+        next_chain()
     far_reach = [far_own]
     far_reach.append(far_own * far_own + turn[0])
     far_reach.append(far_own * far_reach[1] + turn[0] * far_own + turn[1])
-    lists = [far_gain[i] * far_chain[k] for k in range(5) for i in range(3)]
+    lists = [far_gain[i] * far_chain[k] for k in range(4) for i in range(3)]
     squares_of = [far_gain[i] * far_gain[m] for i, m in PAIRS]
     lists += squares_of + [q * far_reach[n] for n in range(3) for q in squares_of]
     block = over_senders(lists)
 
     def squares(power, i, m):
-        at = 15 + power * 6 + PAIRS.index((min(i, m), max(i, m)))
+        at = 12 + power * 6 + PAIRS.index((min(i, m), max(i, m)))
         return block[at : at + 1, :]
 
-    found = solve(lambda k, i: block[3 * k + i : 3 * k + i + 1, :], squares)
-    sent_total = [found[0][i] + found[1][i] + found[2][i] + found[3][i] + found[4][i] for i in range(3)]
+    found = solve(lambda k, i: block[3 * k + i : 3 * k + i + 1, :], squares, [], 4)
     for k in range(4):
         z = sum(far_gain[i] * found[k][i] for i in range(3))
         for s in range(ST):
             b_out[s, k : k + 1, :] = z[s : s + 1, :]
-    for i in range(3):
-        moved = mine[i : i + 1, :] + mine[3 + i : 4 + i, :] - sent_total[i]
-        for s in range(ST):
-            b_out[s, 4 + i : 5 + i, :] = moved
-    for s in range(ST):
-        b_out[s, 7:8, :] = jnp.zeros((1, LANES), F32)
     start(3, lambda b: b_out.at[b // 8], b_in, -1)
 
 
-    label = climb(climb(label_two))
     atom_bond = inverse[0:16, :].astype(I32)
     bond_at = jnp.maximum(atom_bond - 1, 0)
     atom_label = lookup([label[t : t + 1, :] for t in range(BT)], bond_at // LANES, bond_at % LANES)
@@ -523,16 +528,15 @@
 
     unit = jnp.where(is_halo, 1.0, 0.0)
     chain, reach = [right], [unit]
-    for _ in range(3):
+    for _ in range(4):
         nxt = couple([chain[-1], reach[-1]])
         chain.append(nxt[0])
         reach.append(nxt[1])
-    chain.append(couple([chain[-1]])[0])
     base = chain[0] + chain[1] + chain[2] + chain[3] + chain[4]
     grown = [reach[0]]
-    for m in range(1, 4):
+    for m in range(1, 5):
         grown.append(grown[-1] + reach[m])
-    to_atoms([v * g for v in [base] + grown for g in gain])
+    to_atoms([v * g for v in [base] + grown[:4] for g in gain])
     moves = []
     for n in range(15):
         moves.append(difference(n))
@@ -542,40 +546,43 @@
         gathered[n, AT:16, :] = jnp.zeros((16 - AT, LANES), F32)
 
     all_of(3, b_in).wait_recv()
-    back = merge(b_in, 8)
+    back = merge(b_in, 4)
 
     def kind_rows(tiles, k):
         return [tiles[s][k : k + 1, :] for s in range(ST)]
 
     z = [labelled(kind_rows(back, k), label) for k in range(4)]
-    far_pos = [labelled(kind_rows(back, 4 + i), label) for i in range(3)]
     sol_one = base
     for j in range(4):
         sol_one = sol_one + z[j] * grown[3 - j]
     current = None
+    moved = []
     for i in range(3):
-        ahead = head_new[i] - jnp.where(is_halo, far_pos[i], tail_new[i])
+        ahead = head_new[i] - jnp.where(is_halo, 0.0, tail_new[i])
         step = moves[i]
         for j in range(4):
             step = step + z[j] * moves[3 * (1 + 3 - j) + i]
         stretch = ahead - step
+        moved.append(stretch)
         current = stretch * stretch if current is None else current + stretch * stretch
-    target = jnp.sqrt(jnp.maximum(2.0 * length * length - current, 0.5 * length * length))
-    chain_two = [scale * (length - target)]
-    for _ in range(2):
-        chain_two.append(couple([chain_two[-1]])[0])
+
+    def second_right(scale, length, current):
+        target = jnp.sqrt(jnp.maximum(2.0 * length * length - current, 0.5 * length * length))
+        return scale * (length - target)
+
+    chain_two = [jnp.where(is_halo, 0.0, second_right(scale, length, current))]
     tree_sums = times_ones(
-        [unit * v for v in chain_two] + [reach[1] * chain_two[2], reach[2] * chain_two[2]],
+        [reach[k] * chain_two[0] for k in range(1, 5)] + [unit * m for m in moved],
         trees_of[...],
     )
     for s in range(ST):
         c_out[s] = tree_sums[0:8, s * LANES : (s + 1) * LANES]
     start(4, lambda b: c_out.at[b // 8], c_in, 1)
-    for _ in range(2):
+    for _ in range(4):
         chain_two.append(couple([chain_two[-1]])[0])
 
     base_two = chain_two[0] + chain_two[1] + chain_two[2] + chain_two[3] + chain_two[4]
-    to_atoms([base_two * g for g in gain])
+    to_atoms([v * g for v in (base_two, grown[4]) for g in gain])
     mass_atoms = jnp.concatenate(
         [table[j, 6:7, :] for j in range(AT)] + [jnp.zeros((16 - AT, LANES), F32)], axis=0
     )
@@ -593,19 +600,51 @@
         )
         still.append(start_pos - mass_atoms * spread_base)
     trees = [[mass_atoms * gathered[3 * (1 + n) + i] for i in range(3)] for n in range(4)]
+    no_atoms = jnp.zeros((16 - AT, LANES), F32)
+    trees.append(
+        [
+            mass_atoms
+            * jnp.concatenate([sums[j, 3 + i : 4 + i, :] for j in range(AT)] + [no_atoms], axis=0)
+            for i in range(3)
+        ]
+    )
+    all_of(2, a2_in).wait_recv()
+    late = by_kind(merge(a2_in, 4), 3)
+    feed.append(sum(pull[i] * late[i] for i in range(3)))
+    next_chain()
+    far_reach.append(
+        far_own * far_reach[2] + turn[0] * far_reach[1] + turn[1] * far_own + turn[2]
+    )
+    last_sum = over_senders([far_gain[i] * far_chain[4] for i in range(3)])
+    solve(lambda k, i: last_sum[i : i + 1, :], squares, found, 5)
+    sent_total = [
+        found[0][i] + found[1][i] + found[2][i] + found[3][i] + found[4][i] for i in range(3)
+    ]
+    sent_moved = [mine[i : i + 1, :] + mine[3 + i : 4 + i, :] - sent_total[i] for i in range(3)]
     number16 = row16 * LANES + lax.broadcasted_iota(I32, (16, LANES), 1)
     which = jnp.zeros((16, LANES), I32)
     for e in range(SEND):
         which = jnp.where(number16 == sent8[0:1, e : e + 1], e + 1, which)
 
     all_of(4, c_in).wait_recv()
-    far_two = by_kind(merge(c_in, 8), 5)
-    block_two = over_senders([far_gain[i] * far_two[k] for k in range(5) for i in range(3)])
-    found_two = solve(lambda k, i: block_two[3 * k + i : 3 * k + i + 1, :], squares)
+    far_two = by_kind(merge(c_in, 8), 7)
+    apart = [far_two[4 + i] - sent_moved[i] for i in range(3)]
+    far_right_two = second_right(
+        far_scale, far_length, apart[0] * apart[0] + apart[1] * apart[1] + apart[2] * apart[2]
+    )
+    far_right_two = jnp.where(used, far_right_two, 0.0)
+    far_chain_two = [far_right_two]
+    for k in range(4):
+        far_chain_two.append(far_two[k] + far_reach[k] * far_right_two)
+    block_two = over_senders([far_gain[i] * far_chain_two[k] for k in range(5) for i in range(3)])
+    found_two = solve(lambda k, i: block_two[3 * k + i : 3 * k + i + 1, :], squares, [], 5)
     for k in range(4):
         z_two = sum(far_gain[i] * found_two[k][i] for i in range(3))
         for s in range(ST):
             d_out[s, k : k + 1, :] = z_two[s : s + 1, :]
+    for s in range(ST):
+        d_out[s, 4:5, :] = far_right_two[s : s + 1, :]
+        d_out[s, 5:8, :] = jnp.zeros((3, LANES), F32)
     start(5, lambda b: d_out.at[b // 8], d_in, -1)
 
     for i in range(3):
@@ -616,23 +655,24 @@
         still[i] = still[i] - jnp.where(which > 0, own_move, 0.0)
 
     all_of(5, d_in).wait_recv()
-    last = merge(d_in, 4)
+    last = merge(d_in, 8)
     result = sol_one + base_two
-    for j in range(4):
-        result = result + labelled(kind_rows(last, j), label) * grown[3 - j]
+    for j in range(5):
+        result = result + labelled(kind_rows(last, j), label) * grown[3 - j if j < 4 else 4]
     for t in range(BT):
         mult_ref[:, t * LANES : (t + 1) * LANES] = result[t : t + 1, :]
     both = [[back[s][k : k + 1, :] + last[s][k : k + 1, :] for s in range(ST)] for k in range(4)]
-    for j in range(4):
+    both.append(kind_rows(last, 4))
+    for j in range(5):
         z_atom = labelled(both[j], atom_label)
         for i in range(3):
-            still[i] = still[i] - z_atom * trees[3 - j][i]
+            still[i] = still[i] - z_atom * trees[3 - j if j < 4 else 4][i]
     for i in range(3):
         for j in range(AT):
             at = i * ATOMS + j * LANES
             new_ref[:, at : at + LANES] = still[i][j : j + 1, :]
 
-    for stage, target in ((0, r0_in), (1, a_in), (3, b_in), (4, c_in), (5, d_in)):
+    for stage, target in ((0, r0_in), (1, a_in), (2, a2_in), (3, b_in), (4, c_in), (5, d_in)):
         all_of(stage, target).wait_send()
 
 
@@ -662,7 +702,7 @@
                 pltpu.SemaphoreType.DMA((6,)),
                 pltpu.VMEM((AT, 8, LANES), F32),
                 pltpu.VMEM((2, 8, LANES), I32),
-                pltpu.VMEM((7, BONDS, LANES), F32),
+                pltpu.VMEM((8, BONDS, LANES), F32),
                 pltpu.VMEM((BONDS, ATOMS), jnp.bfloat16),
                 pltpu.VMEM((BONDS, ST * LANES), jnp.bfloat16),
                 pltpu.VMEM((BONDS, BONDS), F32),
@@ -675,14 +715,16 @@
                 pltpu.VMEM((15, 16, LANES), F32),
                 pltpu.VMEM((8, LANES), F32),
                 pltpu.VMEM((near, 8, LANES), F32),
+                pltpu.VMEM((ST, 4, LANES), F32),
+                pltpu.VMEM((ST, 4, LANES), F32),
                 pltpu.VMEM((ST, 8, LANES), F32),
                 pltpu.VMEM((ST, 8, LANES), F32),
-                pltpu.VMEM((ST, 4, LANES), F32),
-                pltpu.VMEM((near, 8, LANES), F32),
-                pltpu.VMEM((near, 8, LANES), F32),
                 pltpu.VMEM((near, 8, LANES), F32),
                 pltpu.VMEM((near, 8, LANES), F32),
                 pltpu.VMEM((near, 4, LANES), F32),
+                pltpu.VMEM((near, 4, LANES), F32),
+                pltpu.VMEM((near, 8, LANES), F32),
+                pltpu.VMEM((near, 8, LANES), F32),
                 pltpu.SemaphoreType.DMA((6,)),
                 pltpu.SemaphoreType.DMA((6,)),
             ],

time: 37.2 us -> 35.5 us (0.954)
  Pallas kernels: 36.4 us -> 34.7 us
    pallas_call x1, Pallas kernels: 35.8 us -> 34.1 us  [per_device(): pl.pallas_call(functools.partial(kernel, sizes), out_shape=(pltpu.VMEM((1...]
where the time goes in v4:
time: 35.5 us; the launch traced here: 35.4 us
  Pallas kernels  34.7 us (98%)
  between operations  0.64 us (2%)
    pallas_call x1, Pallas kernels, per_device(): pl.pallas_call(functools.partial(kernel, sizes), out_shape=(pltpu.VMEM((1...  34.1 us

profile of v4, /device:TPU:1, one launch (start us, length us, event | category | flops | bytes accessed | tf_op | source)
XLA Modules:
  0.0 35.4 jit_solution(3123711656645173526)
XLA Ops:
  0.6 34.1 %shard_map.77 = (f32[1,4608]{1,0:T(1,128)S(1)}, f32[1,1024]{1,0:T(1,128)S(1)}) custom-call(f32[3,1,1536]{2,1,0:T(1,128)} %bitcast.8, f32[3,1,1536]{2,1,0:T(1,128)} %bitcast.9, f32[1,1536]{1,0:T(1,128)} %bitcast.10, s32[1,1024]{1,0:T(1,128)} %bitcast.11, s32[1,1024]{1,0:T(1,128)} %bitcast.12, s32[1,16]{1,0:T(1,128)} %bitcast.13), custom_call_target="tpu_custom_call" | custom-call | tf_op jit(solution)/shard_map/pallas_call | solution.py:690
  34.8 0.6 %shard_map.78 = (f32[1,4608]{1,0:T(1,128)}, f32[1,1024]{1,0:T(1,128)}) custom-call(f32[1,4608]{1,0:T(1,128)S(1)} %get-tuple-element.6.new_ref, f32[1,1024]{1,0:T(1,128)S(1)} %get-tuple-element.7.mult_ref), custom_call_target="tpu_custom_call" | custom-call | tf_op jit(solution)/shard_map/pallas_call | solution.py:740

commit v5 on v4

--- a/solution.py
+++ b/solution.py
@@ -17,6 +17,7 @@
 ST = 4
 BLOCKS = [b for b in range(27) if b != 13]
 ROW_OF = {b: n for n, b in enumerate(BLOCKS)}
+FAR_FIRST = sorted(BLOCKS, key=lambda b: (b // 9 == 1) + (b // 3 % 3 == 1) + (b % 3 == 1))
 F32 = jnp.float32
 I32 = jnp.int32
 PAIRS = [(0, 0), (0, 1), (0, 2), (1, 1), (1, 2), (2, 2)]
@@ -69,6 +70,8 @@
     inverse,
     vec,
     rows,
+    split,
+    left_side,
     sums,
     kinds,
     gathered,
@@ -105,16 +108,18 @@
     names = ("gx", "gy", "gz")
     me = [lax.axis_index(n) for n in names]
 
+    near_by = [{o: lax.rem(m + o + n, n) if o else m for o in (-1, 0, 1)} for m, n in zip(me, sizes)]
+
     def device(block, sign):
         offs = (block // 9 - 1, block // 3 % 3 - 1, block % 3 - 1)
-        return tuple(lax.rem(m + sign * o + n, n) for m, o, n in zip(me, offs, sizes))
+        return tuple(axis[sign * o] for axis, o in zip(near_by, offs))
 
     barrier = pltpu.get_barrier_semaphore()
     for b in BLOCKS:
         pl.semaphore_signal(barrier, inc=1, device_id=device(b, 1), device_id_type=MESH)
 
     def start(stage, source, target, sign):
-        for b in BLOCKS:
+        for b in FAR_FIRST:
             pltpu.make_async_remote_copy(
                 src_ref=source(b),
                 dst_ref=target.at[ROW_OF[b]],
@@ -168,10 +173,10 @@
     near = jnp.where(is_halo, 0, tail)
 
     def at_ends(row):
-        tiles = [row(j) for j in range(AT)]
+        lines = [row(j) for j in range(AT)]
         return (
-            lookup(tiles, head // LANES, head % LANES),
-            lookup(tiles, near // LANES, near % LANES),
+            lookup(lines, head // LANES, head % LANES),
+            lookup(lines, near // LANES, near % LANES),
         )
 
     ends = [at_ends(lambda j, k=k: table[j, k : k + 1, :]) for k in range(7)]
@@ -185,35 +190,21 @@
             col = jnp.sum(jnp.where(eye, value[t : t + 1, :], 0.0), axis=1, keepdims=True)
             cols[k, t * LANES : (t + 1) * LANES, :] = jnp.broadcast_to(col, (LANES, LANES))
 
-    to_cols(0, head.astype(F32))
-    to_cols(1, tail.astype(F32))
-
-    def geometry(ahead, behind, mass, ahead_new, behind_new):
-        bond = [p - q for p, q in zip(ahead, behind)]
-        length = jnp.maximum(
-            jnp.sqrt(bond[0] * bond[0] + bond[1] * bond[1] + bond[2] * bond[2]), 0.5
-        )
-        direction = [b / length for b in bond]
-        scale = 1.0 / jnp.sqrt(mass)
-        shift = [p - q for p, q in zip(ahead_new, behind_new)]
-        right = scale * (
-            direction[0] * shift[0] + direction[1] * shift[1] + direction[2] * shift[2] - length
-        )
-        return length, scale, [scale * d for d in direction], right
-
-    near_data = [e[1] for e in ends]
-    _, _, tree_gain, tree_right = geometry(
-        head_data[0:3],
-        near_data[0:3],
-        head_mass + near_data[6],
-        head_new,
-        [near_data[i] + near_data[3 + i] for i in range(3)],
-    )
-    tree_gain = [jnp.where(is_halo, 0.0, g) for g in tree_gain]
-    tree_right = jnp.where(is_halo, 0.0, tree_right)
+    rows[0] = head.astype(F32)
+    rows[1] = tail.astype(F32)
+    both_ends = rows[0] * 2048.0 + rows[1]
+    for t in range(BT):
+        here = slice(t * LANES, (t + 1) * LANES)
+        col = jnp.sum(jnp.where(eye, both_ends[t : t + 1, :], 0.0), axis=1, keepdims=True)
+        col = jnp.broadcast_to(col, (LANES, LANES))
+        heads = jnp.floor(col * (1.0 / 2048.0))
+        for k, value in enumerate((heads, col - 2048.0 * heads)):
+            cols[k, here, :] = value
 
     found_by[...] = jnp.zeros(found_by.shape, F32)
     kinds[...] = jnp.zeros(kinds.shape, F32)
+    split[...] = jnp.zeros(split.shape, F32)
+    half = jnp.bfloat16
 
     def incidence_rows(t, carry):
         here = pl.ds(pl.multiple_of(t * LANES, LANES), LANES)
@@ -238,15 +229,38 @@
             if j < AT:
                 incidence[here, j * LANES : (j + 1) * LANES] = jnp.concatenate(
                     parts, axis=0
-                ).astype(jnp.bfloat16)
+                ).astype(half)
         return carry
 
-    lax.fori_loop(0, 2, incidence_rows, 0)
+    lax.fori_loop(0, BT, incidence_rows, 0)
     pl.semaphore_wait(barrier, len(BLOCKS))
     start(0, lambda b: r0_out, r0_in, -1)
-    lax.fori_loop(2, BT, incidence_rows, 0)
     for j in range(AT + ST):
         inverse[j : j + 1, :] = jnp.sum(found_by[j], axis=0, keepdims=True)
+
+    def geometry(ahead, behind, mass, ahead_new, behind_new):
+        bond = [p - q for p, q in zip(ahead, behind)]
+        length = jnp.maximum(
+            jnp.sqrt(bond[0] * bond[0] + bond[1] * bond[1] + bond[2] * bond[2]), 0.5
+        )
+        direction = [b / length for b in bond]
+        scale = 1.0 / jnp.sqrt(mass)
+        shift = [p - q for p, q in zip(ahead_new, behind_new)]
+        right = scale * (
+            direction[0] * shift[0] + direction[1] * shift[1] + direction[2] * shift[2] - length
+        )
+        return length, scale, [scale * d for d in direction], right
+
+    near_data = [e[1] for e in ends]
+    _, _, tree_gain, tree_right = geometry(
+        head_data[0:3],
+        near_data[0:3],
+        head_mass + near_data[6],
+        head_new,
+        [near_data[i] + near_data[3 + i] for i in range(3)],
+    )
+    tree_gain = [jnp.where(is_halo, 0.0, g) for g in tree_gain]
+    tree_right = jnp.where(is_halo, 0.0, tree_right)
 
     parent = lookup(
         [inverse[j : j + 1, :] for j in range(AT)], near // LANES, near % LANES
@@ -259,10 +273,10 @@
         above = lookup([label[t : t + 1, :] for t in range(BT)], parent // LANES, parent % LANES)
         return jnp.where(has_parent, above, root)
 
-    def put_kinds(values):
+    def put_kinds(values, out=kinds):
         for k, value in enumerate(values):
             for t in range(BT):
-                kinds[t, k : k + 1, :] = value[t : t + 1, :]
+                out[t, k : k + 1, :] = value[t : t + 1, :]
 
     def times_ones(values, matrix):
         height = (len(values) + 15) // 16 * 16
@@ -276,11 +290,16 @@
         product = jnp.dot(parts, matrix, preferred_element_type=F32)
         return product[:height] + (product[height : 2 * height] + product[2 * height :])
 
-    def to_atoms(weighted):
-        total = times_ones(weighted, incidence[...])
-        height = (len(weighted) + 7) // 8 * 8
+    def keep_sums(total, count):
+        height = (count + 7) // 8 * 8
         for j in range(AT):
             sums[j, :height, :] = total[:height, j * LANES : (j + 1) * LANES]
+
+    def to_atoms(weighted):
+        keep_sums(times_ones(weighted, incidence[...]), len(weighted))
+
+    def at_near_of(n):
+        return lookup([sums[j, n : n + 1, :] for j in range(AT)], near // LANES, near % LANES)
 
     def difference(n):
         at_head, at_near = at_ends(lambda j: sums[j, n : n + 1, :])
@@ -290,20 +309,26 @@
     child = jnp.logical_and(label_one > 0.0, jnp.logical_not(is_halo))
     label_two = climb(label_one)
     start_of = [jnp.where(child, g, 0.0) for g in tree_gain]
-    to_atoms(
+    product = times_ones(
         [tree_right * g for g in tree_gain]
-        + [start_of[i] * tree_gain[m] for i, m in PAIRS]
-    )
-    diffs = [difference(n) for n in range(9)]
-    tree_next = tree_right - sum(tree_gain[i] * diffs[i] for i in range(3))
-    start_next = []
-    for i in range(3):
-        start_next.append(
-            start_of[i]
-            - sum(
-                tree_gain[m] * diffs[3 + PAIRS.index((min(i, m), max(i, m)))] for m in range(3)
-            )
-        )
+        + [start_of[i] * tree_gain[m] for i, m in PAIRS],
+        incidence[...],
+    )
+    slots = inverse[AT : AT + ST, :].astype(I32)
+    slot_bond = jnp.maximum(slots - 1, 0)
+    slot_head = lookup(
+        [head[t : t + 1, :].astype(F32) for t in range(BT)],
+        slot_bond // LANES,
+        slot_bond % LANES,
+    ).astype(I32)
+    slot_atoms = []
+    for s in range(ST):
+        at = jnp.broadcast_to(slot_head[s : s + 1, :], (8, LANES))
+        used = jnp.broadcast_to(slots[s : s + 1, :], (8, LANES)) > 0
+        atoms = jnp.zeros((8, LANES), F32)
+        for j in range(AT):
+            atoms = jnp.where(at // LANES == j, take(table[j], at % LANES), atoms)
+        slot_atoms.append(pltpu.roll(jnp.where(used, atoms, 0.0), SEND * 4, axis=1))
     label = climb(climb(label_two))
     to_cols(7, label)
     for s in range(ST):
@@ -311,6 +336,17 @@
         trees_of[:, s * LANES : (s + 1) * LANES] = jnp.where(cols[7] == number, 1.0, 0.0).astype(
             jnp.bfloat16
         )
+    keep_sums(product, 9)
+    diffs = [difference(n) for n in range(3)]
+    tree_next = tree_right - sum(tree_gain[i] * diffs[i] for i in range(3))
+    below = {
+        pair: head_mass * (start_of[pair[0]] * tree_gain[pair[1]]) - near_mass * at_near_of(3 + n)
+        for n, pair in enumerate(PAIRS)
+    }
+    start_next = [
+        start_of[i] - sum(tree_gain[m] * below[min(i, m), max(i, m)] for m in range(3))
+        for i in range(3)
+    ]
     tree_sums = times_ones(
         [start_of[i] * start_of[m] for i, m in PAIRS]
         + [start_of[i] * start_next[m] for i, m in PAIRS]
@@ -320,22 +356,10 @@
         + [y * tree_next for y in start_next],
         trees_of[...],
     )
-    slots = inverse[AT : AT + ST, :].astype(I32)
-    slot_bond = jnp.maximum(slots - 1, 0)
-    slot_head = lookup(
-        [head[t : t + 1, :].astype(F32) for t in range(BT)],
-        slot_bond // LANES,
-        slot_bond % LANES,
-    ).astype(I32)
     for s in range(ST):
-        at = jnp.broadcast_to(slot_head[s : s + 1, :], (8, LANES))
-        used = jnp.broadcast_to(slots[s : s + 1, :], (8, LANES)) > 0
-        atoms = jnp.zeros((8, LANES), F32)
-        for j in range(AT):
-            atoms = jnp.where(at // LANES == j, take(table[j], at % LANES), atoms)
         groups = [tree_sums[8 * n : 8 * n + 8, s * LANES : (s + 1) * LANES] for n in range(4)]
-        groups.append(jnp.where(used, atoms, 0.0))
         turned = [pltpu.roll(g, SEND * n, axis=1) if n else g for n, g in enumerate(groups)]
+        turned.append(slot_atoms[s])
         for b in BLOCKS:
             if b // 8 == s:
                 out = turned[0]
@@ -365,8 +389,21 @@
 
     to_cols(2, head_mass)
     to_cols(3, near_mass)
-    rows[0] = head.astype(F32)
-    rows[1] = tail.astype(F32)
+
+    def shared_rows(t, carry):
+        for part in range(2):
+            here = pl.ds(pl.multiple_of(t * 64 + part * 32, 32), 32)
+            heads, tails = cols[0, here, :], cols[1, here, :]
+            masses, near_masses = cols[2, here, :], cols[3, here, :]
+            minus_near = -near_masses
+            for u in range(BT):
+                head_row, tail_row = rows[0, u : u + 1, :], rows[1, u : u + 1, :]
+                coupling[here, u * LANES : (u + 1) * LANES] = jnp.where(
+                    tails == head_row, minus_near, jnp.where(tails == tail_row, near_masses, 0.0)
+                ) - jnp.where(heads == tail_row, masses, 0.0)
+        return carry
+
+    lax.fori_loop(0, BONDS // 64, shared_rows, 0)
     all_of(0, r0_in).wait_recv()
     halo = merge(r0_in, 8)
     slot_tile, slot_lane = slot // LANES, slot % LANES
@@ -379,32 +416,19 @@
         head_data[0:3], tail_data[0:3], head_mass + tail_data[6], head_new, tail_new
     )
     own = 1.0 - head_mass * (gain[0] * gain[0] + gain[1] * gain[1] + gain[2] * gain[2])
-    for i in range(3):
-        to_cols(4 + i, gain[i])
-    for i in range(3):
-        rows[2 + i] = gain[i]
-
-    def coupling_rows(t, carry):
-        for part in range(2):
-            here = pl.ds(pl.multiple_of(t * 64 + part * 32, 32), 32)
-            heads, tails = cols[0, here, :], cols[1, here, :]
-            masses, near_masses = cols[2, here, :], cols[3, here, :]
-            minus_near = -near_masses
-            gains = [cols[4 + i, here, :] for i in range(3)]
-            for u in range(BT):
-                head_row, tail_row = rows[0, u : u + 1, :], rows[1, u : u + 1, :]
-                shared = jnp.where(
-                    tails == head_row, minus_near, jnp.where(tails == tail_row, near_masses, 0.0)
-                ) - jnp.where(heads == tail_row, masses, 0.0)
-                dots = (
-                    gains[0] * rows[2, u : u + 1, :]
-                    + gains[1] * rows[3, u : u + 1, :]
-                    + gains[2] * rows[4, u : u + 1, :]
-                )
-                coupling[here, u * LANES : (u + 1) * LANES] = shared * dots
-        return carry
-
-    lax.fori_loop(0, BONDS // 64, coupling_rows, 0)
+    high = [g.astype(half).astype(F32) for g in gain]
+    mid = [(g - h).astype(half).astype(F32) for g, h in zip(gain, high)]
+    low = [(g - h - m).astype(half).astype(F32) for g, h, m in zip(gain, high, mid)]
+    put_kinds(high + mid + low + high + mid + high, split.at[0])
+    right_side = jnp.concatenate([split[0, t] for t in range(BT)], axis=1).astype(half)
+    put_kinds(high + high + high + mid + mid + low, split.at[1])
+    for t in range(BT):
+        left_side[t * LANES : (t + 1) * LANES, :] = jnp.transpose(split[1, t]).astype(half)
+
+    for t in range(BT):
+        here = slice(t * LANES, (t + 1) * LANES)
+        dots = jnp.dot(left_side[here, :], right_side, preferred_element_type=F32)
+        coupling[here, :] = coupling[here, :] * dots
 
     def couple(values):
         for n, value in enumerate(values):
@@ -540,11 +564,6 @@
     moves = []
     for n in range(15):
         moves.append(difference(n))
-    for n in range(15):
-        for j in range(AT):
-            gathered[n, j : j + 1, :] = sums[j, n : n + 1, :]
-        gathered[n, AT:16, :] = jnp.zeros((16 - AT, LANES), F32)
-
     all_of(3, b_in).wait_recv()
     back = merge(b_in, 4)
 
@@ -581,6 +600,10 @@
     for _ in range(4):
         chain_two.append(couple([chain_two[-1]])[0])
 
+    for n in range(15):
+        for j in range(AT):
+            gathered[n, j : j + 1, :] = sums[j, n : n + 1, :]
+        gathered[n, AT:16, :] = jnp.zeros((16 - AT, LANES), F32)
     base_two = chain_two[0] + chain_two[1] + chain_two[2] + chain_two[3] + chain_two[4]
     to_atoms([v * g for v in (base_two, grown[4]) for g in gain])
     mass_atoms = jnp.concatenate(
@@ -709,7 +732,9 @@
                 pltpu.VMEM((AT + ST, 8, LANES), F32),
                 pltpu.VMEM((AT + ST, LANES), F32),
                 pltpu.VMEM((2, 8, LANES), F32),
-                pltpu.VMEM((5, 8, LANES), F32),
+                pltpu.VMEM((2, 8, LANES), F32),
+                pltpu.VMEM((2, BT, 32, LANES), F32),
+                pltpu.VMEM((BONDS, 32), jnp.bfloat16),
                 pltpu.VMEM((AT, 16, LANES), F32),
                 pltpu.VMEM((8, 40, LANES), F32),
                 pltpu.VMEM((15, 16, LANES), F32),

time: 35.5 us -> 34.2 us (0.963)
  Pallas kernels: 34.7 us -> 33.4 us
    pallas_call x1, Pallas kernels: 34.1 us -> 32.8 us  [per_device(): pl.pallas_call(functools.partial(kernel, sizes), out_shape=(pltpu.VMEM((1...]
where the time goes in v5:
time: 34.2 us; the launch traced here: 34.1 us
  Pallas kernels  33.4 us (98%)
  between operations  0.64 us (2%)
    pallas_call x1, Pallas kernels, per_device(): pl.pallas_call(functools.partial(kernel, sizes), out_shape=(pltpu.VMEM((1...  32.8 us

profile of v5, /device:TPU:1, one launch (start us, length us, event | category | flops | bytes accessed | tf_op | source)
XLA Modules:
  0.0 34.1 jit_solution(2092991424743862716)
XLA Ops:
  0.6 32.8 %shard_map.77 = (f32[1,4608]{1,0:T(1,128)S(1)}, f32[1,1024]{1,0:T(1,128)S(1)}) custom-call(f32[3,1,1536]{2,1,0:T(1,128)} %bitcast.8, f32[3,1,1536]{2,1,0:T(1,128)} %bitcast.9, f32[1,1536]{1,0:T(1,128)} %bitcast.10, s32[1,1024]{1,0:T(1,128)} %bitcast.11, s32[1,1024]{1,0:T(1,128)} %bitcast.12, s32[1,16]{1,0:T(1,128)} %bitcast.13), custom_call_target="tpu_custom_call" | custom-call | tf_op jit(solution)/shard_map/pallas_call | solution.py:713
  33.4 0.6 %shard_map.78 = (f32[1,4608]{1,0:T(1,128)}, f32[1,1024]{1,0:T(1,128)}) custom-call(f32[1,4608]{1,0:T(1,128)S(1)} %get-tuple-element.6.new_ref, f32[1,1024]{1,0:T(1,128)S(1)} %get-tuple-element.7.mult_ref), custom_call_target="tpu_custom_call" | custom-call | tf_op jit(solution)/shard_map/pallas_call | solution.py:765

commit v6 on v5

--- a/solution.py
+++ b/solution.py
@@ -211,30 +211,31 @@
         heads = cols[0, here, :]
         tails = cols[1, here, :]
         number = (sub128 + (t * LANES + 1)).astype(F32)
-        cuts = [slice(8 * r, 8 * r + 8) for r in range(LANES // 8)]
+        atoms = [(lane8 + j * LANES).astype(F32) for j in range(AT + ST)]
+        numbers_of = [found_by[j] for j in range(AT + ST)]
+        for pair in range(LANES // 16):
+            cuts = [slice(16 * pair + 8 * r, 16 * pair + 8 * r + 8) for r in range(2)]
+            for j in range(AT + ST):
+                parts = []
+                for cut in cuts:
+                    if j < AT:
+                        found = heads[cut] == atoms[j]
+                        parts.append(
+                            jnp.where(found, 1.0, jnp.where(tails[cut] == atoms[j], -1.0, 0.0))
+                        )
+                    else:
+                        found = tails[cut] == atoms[j]
+                    numbers_of[j] = jnp.where(found, number[cut], numbers_of[j])
+                if j < AT:
+                    at = pl.ds(pl.multiple_of(t * LANES + pair * 16, 16), 16)
+                    incidence[at, j * LANES : (j + 1) * LANES] = jnp.concatenate(
+                        parts, axis=0
+                    ).astype(half)
         for j in range(AT + ST):
-            atom = (lane8 + j * LANES).astype(F32)
-            number_of = found_by[j]
-            parts = []
-            for cut in cuts:
-                if j < AT:
-                    found = heads[cut] == atom
-                    parts.append(
-                        jnp.where(found, 1.0, jnp.where(tails[cut] == atom, -1.0, 0.0))
-                    )
-                else:
-                    found = tails[cut] == atom
-                number_of = jnp.where(found, number[cut], number_of)
-            found_by[j] = number_of
-            if j < AT:
-                incidence[here, j * LANES : (j + 1) * LANES] = jnp.concatenate(
-                    parts, axis=0
-                ).astype(half)
+            found_by[j] = numbers_of[j]
         return carry
 
     lax.fori_loop(0, BT, incidence_rows, 0)
-    pl.semaphore_wait(barrier, len(BLOCKS))
-    start(0, lambda b: r0_out, r0_in, -1)
     for j in range(AT + ST):
         inverse[j : j + 1, :] = jnp.sum(found_by[j], axis=0, keepdims=True)
 
@@ -275,8 +276,7 @@
 
     def put_kinds(values, out=kinds):
         for k, value in enumerate(values):
-            for t in range(BT):
-                out[t, k : k + 1, :] = value[t : t + 1, :]
+            out[:, k, :] = value
 
     def times_ones(values, matrix):
         height = (len(values) + 15) // 16 * 16
@@ -314,6 +314,8 @@
         + [start_of[i] * tree_gain[m] for i, m in PAIRS],
         incidence[...],
     )
+    pl.semaphore_wait(barrier, len(BLOCKS))
+    start(0, lambda b: r0_out, r0_in, -1)
     slots = inverse[AT : AT + ST, :].astype(I32)
     slot_bond = jnp.maximum(slots - 1, 0)
     slot_head = lookup(
@@ -450,10 +452,7 @@
     def by_kind(tiles, count):
         for s in range(ST):
             kinds[s, 0 : tiles[s].shape[0], :] = tiles[s]
-        return [
-            jnp.concatenate([kinds[s, k : k + 1, :] for s in range(ST)], axis=0)
-            for k in range(count)
-        ]
+        return [kinds[0:ST, k, :] for k in range(count)]
 
     def over_senders(values):
         lines = [jnp.sum(v, axis=0, keepdims=True) for v in values]

time: 34.2 us -> 33.8 us (0.988)
  Pallas kernels: 33.4 us -> 33 us
    pallas_call x1, Pallas kernels: 32.8 us -> 32.4 us  [per_device(): pl.pallas_call(functools.partial(kernel, sizes), out_shape=(pltpu.VMEM((1...]
where the time goes in v6:
time: 33.8 us; the launch traced here: 33.7 us
  Pallas kernels  33 us (98%)
  between operations  0.64 us (2%)
    pallas_call x1, Pallas kernels, per_device(): pl.pallas_call(functools.partial(kernel, sizes), out_shape=(pltpu.VMEM((1...  32.4 us

profile of v6, /device:TPU:1, one launch (start us, length us, event | category | flops | bytes accessed | tf_op | source)
XLA Modules:
  0.0 33.7 jit_solution(9992917540252498501)
XLA Ops:
  0.6 32.4 %shard_map.77 = (f32[1,4608]{1,0:T(1,128)S(1)}, f32[1,1024]{1,0:T(1,128)S(1)}) custom-call(f32[3,1,1536]{2,1,0:T(1,128)} %bitcast.8, f32[3,1,1536]{2,1,0:T(1,128)} %bitcast.9, f32[1,1536]{1,0:T(1,128)} %bitcast.10, s32[1,1024]{1,0:T(1,128)} %bitcast.11, s32[1,1024]{1,0:T(1,128)} %bitcast.12, s32[1,16]{1,0:T(1,128)} %bitcast.13), custom_call_target="tpu_custom_call" | custom-call | tf_op jit(solution)/shard_map/pallas_call | solution.py:712
  33.1 0.6 %shard_map.78 = (f32[1,4608]{1,0:T(1,128)}, f32[1,1024]{1,0:T(1,128)}) custom-call(f32[1,4608]{1,0:T(1,128)S(1)} %get-tuple-element.6.new_ref, f32[1,1024]{1,0:T(1,128)S(1)} %get-tuple-element.7.mult_ref), custom_call_target="tpu_custom_call" | custom-call | tf_op jit(solution)/shard_map/pallas_call | solution.py:764
